TPU v7x, 32 devices: a whole 2x2x4 slice. The times are simulated.
32 devices in a mesh: row: 4 (over x, core), col: 8 (over z, y).
Axes of the slice: x: 2, y: 2, z: 4, core: 2. Of those that a mesh axis runs over, the one named last changes fastest.
Arguments:
- pooled: bfloat16 [2048, 1152], P(('row', 'col')), may hold values from -32 to 32
- hidden: bfloat16 [2048, 4304], P(('row', 'col')), may hold values from -6 to 6
- text: bfloat16 [2048, 1152], P(('row', 'col')), may hold values from -12 to 12
- weight: float32 [1152, 4304], P('col', 'row'), may hold values from -0.09375 to 0.09375
- row_moment: float32 [1152], P('col'), may hold values from 1e-07 to 1e-05
- col_moment: float32 [4304], P('row'), may hold values from 1e-07 to 1e-05
- log_scale: float32 [], replicated, may hold values from 4.2 to 4.8
- bias: float32 [], replicated, may hold values from -16 to -12
Outputs:
- update: float32 [1152, 4304], P('col', 'row')
- new_row: float32 [1152], P('col')
- new_col: float32 [4304], P('row')
- loss: float32 [], replicated
All inputs are finite; a program needn't handle non-finite values.
Results may differ from a plain program's by a relative error of at most 0.004.
Values may be sent and summed in bfloat16 or wider, within the bound.
A program may use at most 128 MiB of HBM per device.

v0:
```python
import functools

import jax
import jax.numpy as jnp
from jax import lax
from jax.experimental import pallas as pl
from jax.experimental.pallas import tpu as pltpu
from jax.sharding import PartitionSpec as P

EPSILON = 1e-06
DECAY_RATE = 0.8
CLIP_LEVEL = 1.0
FLOOR_VALUE = 1e-30
CORES = 2
LOW = 2
MESH = pl.DeviceIdType.MESH
F32 = jnp.float32
BF16 = jnp.bfloat16


def dot_nt(a, b):
    return lax.dot_general(a, b, (((1,), (1,)), ((), ())), preferred_element_type=F32)


def kernel(
    sizes,
    hs_ref, wh_ref, pool_ref, tx_ref, rm_ref, cm_ref, ls_ref, bias_ref,
    upd_ref, nr_ref, nc_ref, loss_ref,
    hid, wg, txa, part, pre, summed, proj, img_s, img_r, ug_s, ug_r, mg_s, mga, gp, gz_s, gz,
    rsb, csb, stb,
    hid_ss, hid_rs, w_ss, w_rs, tz_ss, tp_ss, t_rs, td_ss, td_rs, pp_ss, pp_rs, p_ss, p_rs, pair_ss, pair_rs,
    mg_ss, mg_rs, g_ss, g_rs, row_ss, row_rs, col_ss, col_rs, st_ss, st_rs,
):
    R, C, X, Z, T, Db, Dp, Fb, chunk = sizes
    L = LOW
    plane = R * L
    devices = R * C
    batch = devices * T
    r = lax.axis_index("row")
    c = lax.axis_index("col")
    z, y = c // L, c % L
    x, core = r // CORES, r % CORES
    q = r * L + y
    finish = []

    def send(src, dst, ss, rs, device, cond=None):
        def make():
            return pltpu.make_async_remote_copy(
                src_ref=src, dst_ref=dst, send_sem=ss, recv_sem=rs,
                device_id=device, device_id_type=MESH,
            )

        if cond is None:
            make().start()
            finish.append(lambda: make().wait_send())
        else:
            pl.when(cond)(lambda: make().start())
            finish.append(lambda: pl.when(cond)(lambda: make().wait_send()))

    def arrived(slot, rs):
        pltpu.make_async_copy(slot, slot, rs).wait()

    def plane_peer(o):
        other = lax.rem(q + o, plane)
        return other, other // L, other % L

    def rows(index, count):
        return pl.ds(pl.multiple_of(index * count, count), count)

    for o in range(1, plane):
        _, r2, y2 = plane_peer(o)
        send(hs_ref.at[r2], hid.at[rows(q, T)], hid_ss.at[o], hid_rs.at[q], (r2, z * L + y2))
    hid[rows(q, T)] = hs_ref[r]

    wg[rows(z, Dp)] = wh_ref[...]
    own_slot = x * C + c
    txa[:, rows(own_slot, T), :] = tx_ref[...]

    def text_place(zs):
        return x * C + zs * L + y

    def neighbours():
        along_x = [(lax.rem(x + o, X), y) for o in range(1, X)]
        return along_x + [(x, lax.rem(y + o, L)) for o in range(1, L)]

    def relay(s):
        for d, direction in enumerate((1, -1)):
            if s == 0 and d:
                continue
            zs = z - direction * s
            has = jnp.logical_and(zs >= 0, zs < Z)
            block = jnp.clip(zs, 0, Z - 1)
            for n, (x2, y2) in enumerate(neighbours()):
                place = x2 * C + block * L + y2
                at = txa.at[:, rows(place, T), :]
                if s:
                    pl.when(has)(lambda: arrived(at, t_rs.at[place]))
                else:
                    arrived(at, t_rs.at[place])
                h = 0 if n < X - 1 else 1
                half = txa.at[h, rows(place, T), :]
                onward = neighbours()[X - 1:] if h == 0 else neighbours()[:X - 1]
                for m, (x3, y3) in enumerate(onward):
                    send(
                        half, half, td_ss.at[d, s, n, m], td_rs.at[place, h],
                        (x3 * CORES + core, z * L + y3), has if s else None,
                    )

    for s in range(Z):
        for d, direction in enumerate((1, -1)):
            zs = z - direction * s
            nz = z + direction
            has = jnp.logical_and(zs >= 0, zs < Z)
            go = jnp.logical_and(has, jnp.logical_and(nz >= 0, nz < Z))
            place = text_place(jnp.clip(zs, 0, Z - 1))
            at = txa.at[:, rows(place, T), :]
            source = tx_ref if s == 0 else at
            if s:
                pl.when(has)(lambda: arrived(at, t_rs.at[place]))
            send(source, at, tz_ss.at[d, s], t_rs.at[place], (r, jnp.clip(nz, 0, Z - 1) * L + y), go)
            if s or d == 0:
                for n, (x2, y2) in enumerate(neighbours()):
                    send(
                        source, at, tp_ss.at[d, s, n], t_rs.at[place],
                        (x2 * CORES + core, z * L + y2), has if s else None,
                    )
        for d, direction in enumerate((1, -1)):
            zs = z - direction * s
            nz = z + direction
            has = jnp.logical_and(zs >= 0, zs < Z)
            go = jnp.logical_and(has, jnp.logical_and(nz >= 0, nz < Z))
            block = jnp.clip(zs, 0, Z - 1)
            at = wg.at[rows(block, Dp)]
            if s:
                pl.when(has)(lambda: arrived(at, w_rs.at[block]))
            send(
                wh_ref if s == 0 else at, at, w_ss.at[d, s], w_rs.at[block],
                (r, jnp.clip(nz, 0, Z - 1) * L + y), go,
            )
        if s:
            relay(s - 1)
    for o in range(1, plane):
        other, _, _ = plane_peer(o)
        arrived(hid.at[rows(other, T)], hid_rs.at[other])

    part[...] = dot_nt(hid[...], wg[...])
    partner = (x * CORES + (1 - core), c)
    for o in range(1, X + 1):
        x2 = lax.rem(x + o, X)
        send(
            part.at[rows(x2 * CORES + 1 - core, L * T)], pre.at[x2],
            pp_ss.at[o], pp_rs.at[x2], partner,
        )
    relay(Z - 1)
    for o in range(1, X + 1):
        x2 = lax.rem(x + o, X)
        arrived(pre.at[x2], pp_rs.at[x2])
        summed[x2] = part[rows(x2 * CORES + core, L * T)] + pre[x2]
        for k in range(L):
            y2 = lax.rem(y + 1 + k, L)
            if o == X and k == L - 1:
                proj[x, y] = summed[x, rows(y, T)]
            else:
                send(
                    summed.at[x2, rows(y2, T)], proj.at[x, y], p_ss.at[o * L + k],
                    p_rs.at[x * L + y], (x2 * CORES + core, z * L + y2),
                )
    for o in range(1, X * L):
        other = lax.rem(x * L + y + o, X * L)
        arrived(proj.at[other // L, other % L], p_rs.at[other])
    mixed = []
    for h in range(L):
        total = proj[0, h]
        for k in range(1, X):
            total = total + proj[k, h]
        mixed.append(pool_ref[h].astype(F32) + total)
    square = sum(jnp.sum(m * m, axis=1, keepdims=True) for m in mixed)
    length = jnp.sqrt(square + EPSILON)
    unit = [m / length for m in mixed]
    for h in range(L):
        img_s[h] = unit[h].astype(BF16)
    send(img_s, img_r, pair_ss.at[0], pair_rs.at[0], partner)

    for ox in range(1, X):
        for oy in range(1, L):
            for zs in range(Z):
                place = lax.rem(x + ox, X) * C + zs * L + lax.rem(y + oy, L)
                for h in range(L):
                    arrived(txa.at[h, rows(place, T), :], td_rs.at[place, h])

    scale = jnp.exp(jnp.full((1, 1), ls_ref[0], F32))
    bias = jnp.full((1, 1), bias_ref[0], F32)
    steps = X * C * T // chunk

    def pairs(images, own):
        halves = [images[h] for h in range(L)]

        def step(i, carry):
            loss, grads = carry
            cut = pl.ds(pl.multiple_of(i * chunk, chunk), chunk)
            texts = [txa[h, cut, :] for h in range(L)]
            logits = scale * sum(dot_nt(halves[h], texts[h]) for h in range(L)) + bias
            if own:
                row_id = lax.broadcasted_iota(jnp.int32, logits.shape, 0) + own_slot * T
                col_id = lax.broadcasted_iota(jnp.int32, logits.shape, 1) + i * chunk
                sign = jnp.where(row_id == col_id, F32(1.0), F32(-1.0))
            else:
                sign = F32(-1.0)
            u = -sign * logits
            e = jnp.exp(-jnp.abs(u))
            loss = loss + jnp.sum(jnp.maximum(u, 0.0) + jnp.log1p(e), axis=1, keepdims=True)
            sig = jnp.where(u >= 0, F32(1.0), e) / (1.0 + e)
            pg = (-sign * sig / batch).astype(BF16)
            grads = tuple(
                grads[h] + jnp.dot(pg, texts[h], preferred_element_type=F32) for h in range(L)
            )
            return loss, grads

        zero = (jnp.zeros((T, 1), F32), tuple(jnp.zeros((T, Z * Dp), F32) for _ in range(L)))
        if steps == 1:
            return step(0, zero)
        return lax.fori_loop(0, steps, step, zero)

    arrived(img_r, pair_rs.at[0])
    loss_b, grads_b = pairs(img_r, False)
    for h in range(L):
        ug_s[h] = scale * grads_b[h]
    send(ug_s, ug_r, pair_ss.at[1], pair_rs.at[1], partner)
    loss_a, grads_a = pairs(img_s, True)
    arrived(ug_r, pair_rs.at[1])
    ug = [scale * grads_a[h] + ug_r[h] for h in range(L)]
    inner = sum(jnp.sum(unit[h] * ug[h], axis=1, keepdims=True) for h in range(L))
    for h in range(L):
        mg_s[h] = ((ug[h] - unit[h] * inner) / length).astype(BF16)
    for o in range(1, X * L):
        other = lax.rem(x * L + y + o, X * L)
        send(
            mg_s.at[other % L], mga.at[rows(q, T)], mg_ss.at[o], mg_rs.at[q],
            ((other // L) * CORES + core, z * L + other % L),
        )
    send(mg_s.at[y], mga.at[rows(q, T)], mg_ss.at[0], mg_rs.at[q], partner)
    mga[rows(q, T)] = mg_s[y]
    for o in range(1, X * L):
        other = lax.rem(x * L + y + o, X * L)
        source = ((other // L) * CORES + core) * L + other % L
        at = mga.at[rows(source, T)]
        arrived(at, mg_rs.at[source])
        send(at, at, mg_ss.at[X * L + o], mg_rs.at[source], partner)
    for o in range(X * L):
        other = lax.rem(x * L + y + o, X * L)
        source = ((other // L) * CORES + 1 - core) * L + other % L
        arrived(mga.at[rows(source, T)], mg_rs.at[source])

    turned = mga[...].T

    def own_part(zd):
        gp[zd] = jnp.dot(turned[zd * Dp:(zd + 1) * Dp], hid[...], preferred_element_type=F32)

    def pass_on(zd, d, direction):
        first = z == (0 if d == 0 else Z - 1)
        before = z < zd if d == 0 else z > zd

        def add():
            arrived(gz.at[d, zd], g_rs.at[d, zd])
            gz_s[zd] = (gp[zd] + gz[d, zd].astype(F32)).astype(BF16)

        def start():
            gz_s[zd] = gp[zd].astype(BF16)

        pl.when(jnp.logical_and(before, first))(start)
        pl.when(jnp.logical_and(before, jnp.logical_not(first)))(add)
        send(
            gz_s.at[zd], gz.at[d, zd], g_ss.at[d, zd], g_rs.at[d, zd],
            (r, jnp.clip(z + direction, 0, Z - 1) * L + y), before,
        )

    for k in range(Z):
        up, down = Z - 1 - k, k
        if k < (Z + 1) // 2:
            own_part(up)
            if down != up:
                own_part(down)
        pass_on(up, 0, 1)
        pass_on(down, 1, -1)
    upd_ref[...] = gp[z][:Db]
    for d in range(2):
        def take():
            arrived(gz.at[d, z], g_rs.at[d, z])
            upd_ref[...] += gz[d, z][:Db].astype(F32)

        pl.when(z > 0 if d == 0 else z < Z - 1)(take)
    g = upd_ref[...]

    sq = g * g + FLOOR_VALUE
    rsb[r] = jnp.sum(sq, axis=1, keepdims=True)
    csb[c] = jnp.sum(sq, axis=0, keepdims=True)
    for o in range(1, C):
        c2 = lax.rem(c + o, C)
        send(csb.at[c], csb.at[c], col_ss.at[o], col_rs.at[c], (r, c2))
    for o in range(1, R):
        r2 = lax.rem(r + o, R)
        send(rsb.at[r], rsb.at[r], row_ss.at[o], row_rs.at[r], (r2, c))
    for o in range(1, R):
        r2 = lax.rem(r + o, R)
        arrived(rsb.at[r2], row_rs.at[r2])
    for o in range(1, C):
        c2 = lax.rem(c + o, C)
        arrived(csb.at[c2], col_rs.at[c2])
    row_sum = sum(rsb[k] for k in range(R))
    col_sum = sum(csb[k] for k in range(C))
    new_row = DECAY_RATE * rm_ref[...] + (1.0 - DECAY_RATE) * row_sum / (R * Fb)
    new_col = DECAY_RATE * cm_ref[...] + (1.0 - DECAY_RATE) * col_sum / (C * Db)
    nr_ref[...] = new_row
    nc_ref[...] = new_col
    raw = g / jnp.sqrt(new_row * new_col)
    upd_ref[...] = raw
    local = jnp.sum(jnp.sum(raw * raw, axis=1, keepdims=True), axis=0, keepdims=True)
    loss_local = jnp.sum(loss_a + loss_b, axis=0, keepdims=True)
    lane = lax.broadcasted_iota(jnp.int32, (1, 128), 1)
    me = r * C + c
    stb[me] = jnp.where(lane == 0, local, loss_local)

    def tell(o, wait):
        other = lax.rem(me + o, devices)
        copy = pltpu.make_async_remote_copy(
            src_ref=stb.at[me], dst_ref=stb.at[me], send_sem=st_ss.at[o], recv_sem=st_rs.at[me],
            device_id=(other // C, other % C), device_id_type=MESH,
        )
        if wait:
            copy.wait_send()
            arrived(stb.at[other], st_rs.at[other])
        else:
            copy.start()

    def tell_start(o, _):
        tell(o, False)
        return _

    def tell_wait(o, _):
        tell(o, True)
        return _

    lax.fori_loop(1, devices, tell_start, 0)
    lax.fori_loop(1, devices, tell_wait, 0)
    totals = jnp.sum(stb[...], axis=0)
    rms = jnp.sqrt(totals[:, 0:1] / (C * Db * R * Fb))
    upd_ref[...] = upd_ref[...] / jnp.maximum(1.0, rms / CLIP_LEVEL)
    loss_ref[...] = totals / batch
    for wait in finish:
        wait()


def per_device(pooled, hidden, text, weight, row_moment, col_moment, log_scale, bias):
    R, C = lax.axis_size("row"), lax.axis_size("col")
    L, X, Z = LOW, R // CORES, C // LOW
    T, D = pooled.shape
    Db, Fb = weight.shape
    Dp = -(-Db // 16) * 16
    F2 = Z * Dp
    plane = R * L
    texts = X * C * T
    chunk = min(texts, 512)

    def by_half(a):
        a = a.reshape(T, Z, L, Db).transpose(2, 0, 1, 3)
        if Dp != Db:
            a = jnp.pad(a, ((0, 0), (0, 0), (0, 0), (0, Dp - Db)))
        return a.reshape(L, T, F2)

    hs = hidden.reshape(T, R, Fb).transpose(1, 0, 2)
    wh = weight.astype(BF16)
    if Dp != Db:
        wh = jnp.pad(wh, ((0, Dp - Db), (0, 0)))
    tf = text.astype(F32)
    tn = (tf / jnp.sqrt(jnp.sum(tf * tf, axis=1, keepdims=True) + EPSILON)).astype(BF16)
    sizes = (R, C, X, Z, T, Db, Dp, Fb, chunk)
    vmem = pl.BlockSpec(memory_space=pltpu.VMEM)
    smem = pl.BlockSpec(memory_space=pltpu.SMEM)
    dma = lambda *s: pltpu.SemaphoreType.DMA(s)
    upd, nr, nc, loss = pl.pallas_call(
        functools.partial(kernel, sizes),
        out_shape=(
            jax.ShapeDtypeStruct((Db, Fb), F32),
            jax.ShapeDtypeStruct((Db, 1), F32),
            jax.ShapeDtypeStruct((1, Fb), F32),
            jax.ShapeDtypeStruct((1, 128), F32),
        ),
        in_specs=[vmem] * 6 + [smem] * 2,
        out_specs=(vmem,) * 4,
        scratch_shapes=[
            pltpu.VMEM((plane * T, Fb), BF16),
            pltpu.VMEM((F2, Fb), BF16),
            pltpu.VMEM((L, texts, F2), BF16),
            pltpu.VMEM((plane * T, F2), F32),
            pltpu.VMEM((X, L * T, F2), F32),
            pltpu.VMEM((X, L * T, F2), F32),
            pltpu.VMEM((X, L, T, F2), F32),
            pltpu.VMEM((L, T, F2), BF16),
            pltpu.VMEM((L, T, F2), BF16),
            pltpu.VMEM((L, T, F2), F32),
            pltpu.VMEM((L, T, F2), F32),
            pltpu.VMEM((L, T, F2), BF16),
            pltpu.VMEM((plane * T, F2), BF16),
            pltpu.VMEM((Z, Dp, Fb), F32),
            pltpu.VMEM((Z, Dp, Fb), BF16),
            pltpu.VMEM((2, Z, Dp, Fb), BF16),
            pltpu.VMEM((R, Db, 1), F32),
            pltpu.VMEM((C, 1, Fb), F32),
            pltpu.VMEM((R * C, 1, 128), F32),
            dma(plane), dma(plane), dma(2, Z), dma(Z), dma(2, Z), dma(2, Z, X + L), dma(X * C),
            dma(2, Z, X + L, X + L), dma(X * C, L), dma(X + 1), dma(X), dma(X * L + L), dma(X * L),
            dma(2), dma(2), dma(plane), dma(plane), dma(2, Z), dma(2, Z),
            dma(R), dma(R), dma(C), dma(C), dma(R * C), dma(R * C),
        ],
        compiler_params=pltpu.CompilerParams(
            has_side_effects=True, vmem_limit_bytes=60 * 1024 * 1024
        ),
    )(
        hs, wh, by_half(pooled), by_half(tn), row_moment[:, None], col_moment[None, :],
        log_scale[None], bias[None],
    )
    return upd, nr[:, 0], nc[0], loss[0, 1]


def solution(mesh):
    return jax.shard_map(
        per_device,
        mesh=mesh,
        in_specs=(
            P(("row", "col"), None),
            P(("row", "col"), None),
            P(("row", "col"), None),
            P("col", "row"),
            P("col"),
            P("row"),
            P(),
            P(),
        ),
        out_specs=(P("col", "row"), P("col"), P("row"), P()),
        check_vma=False,
    )
```

profile of v0, /device:TPU:0, one launch (start us, length us, event | category | flops | bytes accessed | tf_op | source)
XLA Modules:
  0.0 132.7 jit_solution(8593903348445643592)
XLA Ops:
  2.0 1.0 fusion
  3.1 0.0 copy-start.6
  3.1 0.6 broadcast_in_dim.14.cm_ref
  3.7 0.1 copy-done.6
  3.7 0.7 copy.17.rm_ref
  4.5 0.1 fusion.1
  4.6 0.4 reshape.32
  5.0 0.1 copy.22
  5.1 0.0 copy-start.3
  5.1 0.9 reshape.33.tx_ref
  5.9 0.0 copy-done.3
  6.0 0.4 reshape.30
  6.3 0.1 copy.23
  6.5 0.9 reshape.31.pool_ref
  7.3 0.8 convert_element_type.9.wh_ref
  8.1 0.4 copy-done.2
  8.5 0.4 reshape.29
  8.9 0.9 copy.21
  9.8 117.5 %shard_map.111 = (f32[144,1076]{1,0:T(8,128)}, f32[144,1]{1,0:T(8,128)}, f32[1,1076]{1,0:T(1,128)}, f32[1,128]{1,0:T(1,128)}) custom-call(bf16[4,64,1076]{2,1,0:T(8,128)(2,1)} %bitcast.15, bf16[144,1076]{1,0:T(8,128)(2,1)} %convert_element_type.9.wh_ref, bf16[2,64,576]{2,1,0:T(8,128)(2,1)} %reshape.31.pool_ref, bf16[2,64,576]{2,1,0:T(8,128)(2,1)} %reshape.33.tx_ref, ...), custom_call_target="tpu_custom_call" | custom-call | tf_op jit(solution)/shard_map/pallas_call | solution.py:380
  127.4 0.6 copy-done.7
  127.9 0.6 slice.3
  128.5 1.6 %reduce = f32[144]{0:T(256)} reduce(f32[144,1]{1,0:T(8,128)} %get-tuple-element.9, f32[]{:T(128)} %constant.4), dimensions={1}, to_apply=%get-tuple-element.9.reduce_sub_computation | reduce | bytes 1156 | tf_op jit(solution)/shard_map/pallas_call | solution.py:380
  130.1 0.6 reduce.1
  130.7 2.0 %copy.27 = f32[144,1076]{1,0:T(8,128)} copy(f32[144,1076]{1,0:T(8,128)} %get-tuple-element.16) | data formatting | bytes 1239552
  (11 shorter events, 0.0 us)
Async XLA Ops:
  0.6 3.9 %copy-start.1 = (bf16[64,1152]{1,0:T(8,128)(2,1)S(1)}, bf16[64,1152]{1,0:T(8,128)(2,1)}, u32[]{:S(2)}) copy-start(bf16[64,1152]{1,0:T(8,128)(2,1)} %param.10) | copy-start | bytes 442372
  2.0 1.1 copy-start.4
  3.1 0.7 copy-start.6
  5.1 0.9 copy-start.3
  6.0 1.3 %copy-start = (f32[144,1076]{1,0:T(8,128)S(1)}, f32[144,1076]{1,0:T(8,128)}, u32[]{:S(2)}) copy-start(f32[144,1076]{1,0:T(8,128)} %param.11) | copy-start | bytes 1859332
  7.3 1.2 copy-start.2
  127.3 0.6 copy-start.7
  128.5 1.6 %copy-start.5 = (f32[1,1076]{1,0:T(1,128)S(1)}, f32[1,1076]{1,0:T(1,128)}, u32[]{:S(2)}) copy-start(f32[1,1076]{1,0:T(1,128)} %get-tuple-element.10) | copy-start | bytes 12916
where the time goes:
time: 133 us
  Pallas kernels  118 us (89%)
  local copies, waits for them, and re-layouts  9 us (7%)
  other arithmetic  4.1 us (3%)
  between operations  2.08 us (2%)
    pallas_call x1, Pallas kernels, per_device(): pl.pallas_call(functools.partial(kernel, sizes), out_shape=(jax.ShapeDtyp...  118 us
    unnamed x17, local copies, waits for them, and re-layouts  3.11 us

commit v1 on v0

--- a/solution.py
+++ b/solution.py
@@ -24,14 +24,15 @@
 
 def kernel(
     sizes,
-    hs_ref, wh_ref, pool_ref, tx_ref, rm_ref, cm_ref, ls_ref, bias_ref,
+    hid_in, w_in, pool_in, text_in, rm_in, cm_in, ls_ref, bias_ref,
     upd_ref, nr_ref, nc_ref, loss_ref,
-    hid, wg, txa, part, pre, summed, proj, img_s, img_r, ug_s, ug_r, mg_s, mga, gp, gz_s, gz,
-    rsb, csb, stb,
+    hv, wv, pv, tv, rmv, cmv, hs, pool, rmc,
+    hid, wg, txa, part, pre, summed, proj, img_s, img_r, ug_s, ug_r, mg_s, mga, turned, gp, gz_s, gz,
+    rsb, csb, stb, ld,
     hid_ss, hid_rs, w_ss, w_rs, tz_ss, tp_ss, t_rs, td_ss, td_rs, pp_ss, pp_rs, p_ss, p_rs, pair_ss, pair_rs,
     mg_ss, mg_rs, g_ss, g_rs, row_ss, row_rs, col_ss, col_rs, st_ss, st_rs,
 ):
-    R, C, X, Z, T, Db, Dp, Fb, chunk = sizes
+    R, C, X, Z, T, Db, Dp, Fb, chunk, K = sizes
     L = LOW
     plane = R * L
     devices = R * C
@@ -42,6 +43,25 @@
     x, core = r // CORES, r % CORES
     q = r * L + y
     finish = []
+    me = r * C + c
+    Dc = Dp // K
+
+    loads = [
+        pltpu.make_async_copy(src, dst, ld.at[i])
+        for i, (src, dst) in enumerate(
+            ((w_in, wv), (hid_in, hv), (text_in, tv), (pool_in, pv), (rm_in, rmv), (cm_in, cmv))
+        )
+    ]
+    for load in loads:
+        load.start()
+    barrier = pltpu.get_barrier_semaphore()
+
+    def greet(o, _):
+        other = lax.rem(me + o, devices)
+        pl.semaphore_signal(barrier, inc=1, device_id=(other // C, other % C), device_id_type=MESH)
+        return _
+
+    lax.fori_loop(1, devices, greet, 0)
 
     def send(src, dst, ss, rs, device, cond=None):
         def make():
@@ -67,14 +87,35 @@
     def rows(index, count):
         return pl.ds(pl.multiple_of(index * count, count), count)
 
+    def by_half(value, store):
+        for h in range(L):
+            for k in range(Z):
+                at = (k * L + h) * Db
+                store(h, k * Dp, value[:, at:at + Db])
+
+    own_slot = x * C + c
+    loads[0].wait()
+    if Dp != Db:
+        wg[rows(z, Dp)] = jnp.zeros((Dp, Fb), BF16)
+        txa[:, rows(own_slot, T), :] = jnp.zeros((L, T, Z * Dp), BF16)
+        pool[...] = jnp.zeros(pool.shape, F32)
+    wg[pl.ds(pl.multiple_of(z * Dp, Dp), Db)] = wv[...].astype(BF16)
+    loads[1].wait()
+    for k in range(R):
+        hs[k] = hv[:, k * Fb:(k + 1) * Fb]
+    hid[rows(q, T)] = hs[r]
+    loads[2].wait()
+    tf = tv[...].astype(F32)
+    tn = tf / jnp.sqrt(jnp.sum(tf * tf, axis=1, keepdims=True) + EPSILON)
+
+    def put_text(h, at, value):
+        txa[h, rows(own_slot, T), at:at + Db] = value.astype(BF16)
+
+    by_half(tn, put_text)
+    pl.semaphore_wait(barrier, devices - 1)
     for o in range(1, plane):
         _, r2, y2 = plane_peer(o)
-        send(hs_ref.at[r2], hid.at[rows(q, T)], hid_ss.at[o], hid_rs.at[q], (r2, z * L + y2))
-    hid[rows(q, T)] = hs_ref[r]
-
-    wg[rows(z, Dp)] = wh_ref[...]
-    own_slot = x * C + c
-    txa[:, rows(own_slot, T), :] = tx_ref[...]
+        send(hs.at[r2], hid.at[rows(q, T)], hid_ss.at[o], hid_rs.at[q], (r2, z * L + y2))
 
     def text_place(zs):
         return x * C + zs * L + y
@@ -114,14 +155,13 @@
             go = jnp.logical_and(has, jnp.logical_and(nz >= 0, nz < Z))
             place = text_place(jnp.clip(zs, 0, Z - 1))
             at = txa.at[:, rows(place, T), :]
-            source = tx_ref if s == 0 else at
             if s:
                 pl.when(has)(lambda: arrived(at, t_rs.at[place]))
-            send(source, at, tz_ss.at[d, s], t_rs.at[place], (r, jnp.clip(nz, 0, Z - 1) * L + y), go)
+            send(at, at, tz_ss.at[d, s], t_rs.at[place], (r, jnp.clip(nz, 0, Z - 1) * L + y), go)
             if s or d == 0:
                 for n, (x2, y2) in enumerate(neighbours()):
                     send(
-                        source, at, tp_ss.at[d, s, n], t_rs.at[place],
+                        at, at, tp_ss.at[d, s, n], t_rs.at[place],
                         (x2 * CORES + core, z * L + y2), has if s else None,
                     )
         for d, direction in enumerate((1, -1)):
@@ -134,11 +174,23 @@
             if s:
                 pl.when(has)(lambda: arrived(at, w_rs.at[block]))
             send(
-                wh_ref if s == 0 else at, at, w_ss.at[d, s], w_rs.at[block],
+                at, at, w_ss.at[d, s], w_rs.at[block],
                 (r, jnp.clip(nz, 0, Z - 1) * L + y), go,
             )
         if s:
             relay(s - 1)
+        else:
+            loads[3].wait()
+
+            def put_pool(h, at, value):
+                pool[h, :, at:at + Db] = value
+
+            by_half(pv[...].astype(F32), put_pool)
+            loads[4].wait()
+            loads[5].wait()
+            eye = lax.broadcasted_iota(jnp.int32, (Db, Db), 0) == lax.broadcasted_iota(jnp.int32, (Db, Db), 1)
+            line = jnp.broadcast_to(rmv[...].reshape(1, Db), (Db, Db))
+            rmc[...] = jnp.sum(jnp.where(eye, line, 0.0), axis=1, keepdims=True)
     for o in range(1, plane):
         other, _, _ = plane_peer(o)
         arrived(hid.at[rows(other, T)], hid_rs.at[other])
@@ -173,7 +225,7 @@
         total = proj[0, h]
         for k in range(1, X):
             total = total + proj[k, h]
-        mixed.append(pool_ref[h].astype(F32) + total)
+        mixed.append(pool[h] + total)
     square = sum(jnp.sum(m * m, axis=1, keepdims=True) for m in mixed)
     length = jnp.sqrt(square + EPSILON)
     unit = [m / length for m in mixed]
@@ -251,45 +303,68 @@
         source = ((other // L) * CORES + 1 - core) * L + other % L
         arrived(mga.at[rows(source, T)], mg_rs.at[source])
 
-    turned = mga[...].T
+    turned[...] = mga[...].T
 
     def own_part(zd):
-        gp[zd] = jnp.dot(turned[zd * Dp:(zd + 1) * Dp], hid[...], preferred_element_type=F32)
-
-    def pass_on(zd, d, direction):
-        first = z == (0 if d == 0 else Z - 1)
-        before = z < zd if d == 0 else z > zd
-
-        def add():
-            arrived(gz.at[d, zd], g_rs.at[d, zd])
-            gz_s[zd] = (gp[zd] + gz[d, zd].astype(F32)).astype(BF16)
-
-        def start():
-            gz_s[zd] = gp[zd].astype(BF16)
-
-        pl.when(jnp.logical_and(before, first))(start)
-        pl.when(jnp.logical_and(before, jnp.logical_not(first)))(add)
-        send(
-            gz_s.at[zd], gz.at[d, zd], g_ss.at[d, zd], g_rs.at[d, zd],
-            (r, jnp.clip(z + direction, 0, Z - 1) * L + y), before,
+        gp[zd] = jnp.dot(turned[rows(zd, Dp)], hid[...], preferred_element_type=F32)
+
+    def pieces(tau, d):
+        place = z if d == 0 else Z - 1 - z
+        i = tau - 2 * place
+        zd = jnp.clip(i, 0, Z * K - 1) // K
+        k = jnp.clip(i, 0, Z * K - 1) % K
+        zd = Z - 1 - zd if d == 0 else zd
+        beyond = zd > z if d == 0 else zd < z
+        ready = jnp.logical_and(i >= 0, i < Z * K)
+        cut = rows(k, Dc)
+        copy = pltpu.make_async_remote_copy(
+            src_ref=gz_s.at[zd, cut], dst_ref=gz.at[d, zd, cut],
+            send_sem=g_ss.at[d, zd, k], recv_sem=g_rs.at[d, zd, k],
+            device_id=(r, jnp.clip(z + (1 if d == 0 else -1), 0, Z - 1) * L + y), device_id_type=MESH,
         )
-
-    for k in range(Z):
-        up, down = Z - 1 - k, k
-        if k < (Z + 1) // 2:
-            own_part(up)
-            if down != up:
-                own_part(down)
-        pass_on(up, 0, 1)
-        pass_on(down, 1, -1)
-    upd_ref[...] = gp[z][:Db]
-    for d in range(2):
-        def take():
-            arrived(gz.at[d, z], g_rs.at[d, z])
-            upd_ref[...] += gz[d, z][:Db].astype(F32)
-
-        pl.when(z > 0 if d == 0 else z < Z - 1)(take)
-    g = upd_ref[...]
+        return place, zd, k, cut, jnp.logical_and(ready, beyond), jnp.logical_and(ready, zd == z), copy
+
+    def step(tau, _):
+        for d in range(2):
+            place, zd, k, cut, passing, ending, copy = pieces(tau, d)
+            at = gz.at[d, zd, cut]
+
+            def first():
+                gz_s[zd, cut] = gp[zd, cut].astype(BF16)
+                copy.start()
+
+            def onward():
+                arrived(at, g_rs.at[d, zd, k])
+                gz_s[zd, cut] = (gp[zd, cut] + at[...].astype(F32)).astype(BF16)
+                copy.start()
+
+            def last():
+                arrived(at, g_rs.at[d, zd, k])
+                gp[zd, cut] = gp[zd, cut] + at[...].astype(F32)
+
+            pl.when(jnp.logical_and(passing, place == 0))(first)
+            pl.when(jnp.logical_and(passing, place > 0))(onward)
+            pl.when(jnp.logical_and(ending, place > 0))(last)
+        return _
+
+    def drain(tau, _):
+        for d in range(2):
+            passing, copy = pieces(tau, d)[4::2]
+            pl.when(passing)(lambda: copy.wait_send())
+        return _
+
+    steps_g = max((Z - 1) * K + 1, K - 1 + 2 * (Z - 1)) + 1
+    head = min(K, 2)
+
+    def order(k):
+        return jnp.where(z < (Z + 1) // 2, Z - 1 - k, k)
+
+    own_part(order(0))
+    lax.fori_loop(0, head, step, 0)
+    for k in range(1, Z):
+        own_part(order(k))
+    lax.fori_loop(head, steps_g, step, 0)
+    g = gp[z][:Db]
 
     sq = g * g + FLOOR_VALUE
     rsb[r] = jnp.sum(sq, axis=1, keepdims=True)
@@ -308,16 +383,15 @@
         arrived(csb.at[c2], col_rs.at[c2])
     row_sum = sum(rsb[k] for k in range(R))
     col_sum = sum(csb[k] for k in range(C))
-    new_row = DECAY_RATE * rm_ref[...] + (1.0 - DECAY_RATE) * row_sum / (R * Fb)
-    new_col = DECAY_RATE * cm_ref[...] + (1.0 - DECAY_RATE) * col_sum / (C * Db)
-    nr_ref[...] = new_row
-    nc_ref[...] = new_col
+    new_row = DECAY_RATE * rmc[...] + (1.0 - DECAY_RATE) * row_sum / (R * Fb)
+    new_col = DECAY_RATE * cmv[...].reshape(1, Fb) + (1.0 - DECAY_RATE) * col_sum / (C * Db)
+    nr_ref[...] = jnp.sum(jnp.where(eye, new_row, 0.0), axis=0)
+    nc_ref[...] = new_col[0]
     raw = g / jnp.sqrt(new_row * new_col)
     upd_ref[...] = raw
     local = jnp.sum(jnp.sum(raw * raw, axis=1, keepdims=True), axis=0, keepdims=True)
     loss_local = jnp.sum(loss_a + loss_b, axis=0, keepdims=True)
     lane = lax.broadcasted_iota(jnp.int32, (1, 128), 1)
-    me = r * C + c
     stb[me] = jnp.where(lane == 0, local, loss_local)
 
     def tell(o, wait):
@@ -345,7 +419,8 @@
     totals = jnp.sum(stb[...], axis=0)
     rms = jnp.sqrt(totals[:, 0:1] / (C * Db * R * Fb))
     upd_ref[...] = upd_ref[...] / jnp.maximum(1.0, rms / CLIP_LEVEL)
-    loss_ref[...] = totals / batch
+    loss_ref[0] = jnp.sum(jnp.where(lane == 1, totals, 0.0)) / batch
+    lax.fori_loop(0, steps_g, drain, 0)
     for wait in finish:
         wait()
 
@@ -361,19 +436,8 @@
     texts = X * C * T
     chunk = min(texts, 512)
 
-    def by_half(a):
-        a = a.reshape(T, Z, L, Db).transpose(2, 0, 1, 3)
-        if Dp != Db:
-            a = jnp.pad(a, ((0, 0), (0, 0), (0, 0), (0, Dp - Db)))
-        return a.reshape(L, T, F2)
-
-    hs = hidden.reshape(T, R, Fb).transpose(1, 0, 2)
-    wh = weight.astype(BF16)
-    if Dp != Db:
-        wh = jnp.pad(wh, ((0, Dp - Db), (0, 0)))
-    tf = text.astype(F32)
-    tn = (tf / jnp.sqrt(jnp.sum(tf * tf, axis=1, keepdims=True) + EPSILON)).astype(BF16)
-    sizes = (R, C, X, Z, T, Db, Dp, Fb, chunk)
+    K = 3 if Dp % 48 == 0 else 1
+    sizes = (R, C, X, Z, T, Db, Dp, Fb, chunk, K)
     vmem = pl.BlockSpec(memory_space=pltpu.VMEM)
     smem = pl.BlockSpec(memory_space=pltpu.SMEM)
     dma = lambda *s: pltpu.SemaphoreType.DMA(s)
@@ -381,13 +445,22 @@
         functools.partial(kernel, sizes),
         out_shape=(
             jax.ShapeDtypeStruct((Db, Fb), F32),
-            jax.ShapeDtypeStruct((Db, 1), F32),
-            jax.ShapeDtypeStruct((1, Fb), F32),
-            jax.ShapeDtypeStruct((1, 128), F32),
+            jax.ShapeDtypeStruct((Db,), F32),
+            jax.ShapeDtypeStruct((Fb,), F32),
+            jax.ShapeDtypeStruct((1,), F32),
         ),
-        in_specs=[vmem] * 6 + [smem] * 2,
-        out_specs=(vmem,) * 4,
+        in_specs=[pl.BlockSpec(memory_space=pl.ANY)] * 6 + [smem] * 2,
+        out_specs=(vmem,) * 3 + (smem,),
         scratch_shapes=[
+            pltpu.VMEM((T, R * Fb), BF16),
+            pltpu.VMEM((Db, Fb), F32),
+            pltpu.VMEM((T, D), BF16),
+            pltpu.VMEM((T, D), BF16),
+            pltpu.VMEM((Db,), F32),
+            pltpu.VMEM((Fb,), F32),
+            pltpu.VMEM((R, T, Fb), BF16),
+            pltpu.VMEM((L, T, F2), F32),
+            pltpu.VMEM((Db, 1), F32),
             pltpu.VMEM((plane * T, Fb), BF16),
             pltpu.VMEM((F2, Fb), BF16),
             pltpu.VMEM((L, texts, F2), BF16),
@@ -401,25 +474,26 @@
             pltpu.VMEM((L, T, F2), F32),
             pltpu.VMEM((L, T, F2), BF16),
             pltpu.VMEM((plane * T, F2), BF16),
+            pltpu.VMEM((F2, plane * T), BF16),
             pltpu.VMEM((Z, Dp, Fb), F32),
             pltpu.VMEM((Z, Dp, Fb), BF16),
             pltpu.VMEM((2, Z, Dp, Fb), BF16),
             pltpu.VMEM((R, Db, 1), F32),
             pltpu.VMEM((C, 1, Fb), F32),
             pltpu.VMEM((R * C, 1, 128), F32),
+            dma(6),
             dma(plane), dma(plane), dma(2, Z), dma(Z), dma(2, Z), dma(2, Z, X + L), dma(X * C),
             dma(2, Z, X + L, X + L), dma(X * C, L), dma(X + 1), dma(X), dma(X * L + L), dma(X * L),
-            dma(2), dma(2), dma(plane), dma(plane), dma(2, Z), dma(2, Z),
+            dma(2), dma(2), dma(plane), dma(plane), dma(2, Z, K), dma(2, Z, K),
             dma(R), dma(R), dma(C), dma(C), dma(R * C), dma(R * C),
         ],
         compiler_params=pltpu.CompilerParams(
-            has_side_effects=True, vmem_limit_bytes=60 * 1024 * 1024
+            has_side_effects=True, collective_id=0, vmem_limit_bytes=60 * 1024 * 1024
         ),
     )(
-        hs, wh, by_half(pooled), by_half(tn), row_moment[:, None], col_moment[None, :],
-        log_scale[None], bias[None],
+        hidden, weight, pooled, text, row_moment, col_moment, log_scale[None], bias[None],
     )
-    return upd, nr[:, 0], nc[0], loss[0, 1]
+    return upd, nr, nc, loss[0]
 
 
 def solution(mesh):

time: 133 us -> 111 us (0.83)
  Pallas kernels: 118 us -> 104 us
  local copies, waits for them, and re-layouts: 9 us -> 3.15 us
  other arithmetic: 4.1 us -> 0 us
  between operations: 2.08 us -> 3.75 us
    pallas_call x1, Pallas kernels: 118 us -> 104 us  [per_device(): pl.pallas_call(functools.partial(kernel, sizes), out_shape=(jax.ShapeDtyp...]
    reshape x8 -> x0, local copies, waits for them, and re-layouts: 3.97 us -> none  [the longest x2 1.73 us: by_half(): return a.reshape(L, T, F2)]
    pallas_call x2 -> x0, other arithmetic: 2.19 us -> none  [per_device(): pl.pallas_call(functools.partial(kernel, sizes), out_shape=(jax.ShapeDtyp...]
    broadcast_in_dim x2 -> x0, local copies, waits for them, and re-layouts: 1.34 us -> none  [the longest x1 0.75 us: per_device(): row_moment[:, None]]
    unnamed x17 -> x7, local copies, waits for them, and re-layouts: 3.11 us -> 3.15 us
where the time goes in v1:
time: 111 us
  Pallas kernels  104 us (94%)
  between operations  3.75 us (3%)
  local copies, waits for them, and re-layouts  3.15 us (3%)
    pallas_call x1, Pallas kernels, per_device(): pl.pallas_call(functools.partial(kernel, sizes), out_shape=(jax.ShapeDtyp...  104 us
    unnamed x7, local copies, waits for them, and re-layouts  3.15 us

profile of v1, /device:TPU:0, one launch (start us, length us, event | category | flops | bytes accessed | tf_op | source)
XLA Modules:
  0.0 110.5 jit_solution(1618413184888870747)
XLA Ops:
  1.9 103.6 %shard_map.111 = (f32[144,1076]{1,0:T(8,128)}, f32[144]{0:T(256)}, f32[1076]{0:T(1024)}, f32[1]{0:T(128)}) custom-call(bf16[64,4304]{1,0:T(8,128)(2,1)} %hid_in.1, f32[144,1076]{1,0:T(8,128)} %w_in.1, bf16[64,1152]{1,0:T(8,128)(2,1)} %pool_in.1, bf16[64,1152]{1,0:T(8,128)(2,1)} %text_in.1, f32[144]{0:T(256)} %rm_in.1, f32[1076]{0:T(1024)} %cm_in.1, ...), custom_call_target="tpu_custom_call" | custom-call | tf_op jit(solution)/shard_map/pallas_call | solution.py:444
  105.6 0.0 copy-start.1
  105.6 0.0 copy-start
  105.6 2.0 %copy.18 = f32[144,1076]{1,0:T(8,128)} copy(f32[144,1076]{1,0:T(8,128)} %get-tuple-element.16) | data formatting | bytes 1239552
  107.6 0.0 copy-done.1
  107.6 0.6 copy.19
  108.1 0.0 copy-done
  108.1 0.6 copy.20
Async XLA Ops:
  105.6 2.0 %copy-start.1 = (f32[144]{0:T(256)S(1)}, f32[144]{0:T(256)}, u32[]{:S(2)}) copy-start(f32[144]{0:T(256)} %get-tuple-element.17) | copy-start | bytes 1732
  105.6 2.6 %copy-start = (f32[1076]{0:T(1024)S(1)}, f32[1076]{0:T(1024)}, u32[]{:S(2)}) copy-start(f32[1076]{0:T(1024)} %get-tuple-element.18) | copy-start | bytes 12916

commit v2 on v1

--- a/solution.py
+++ b/solution.py
@@ -32,7 +32,7 @@
     hid_ss, hid_rs, w_ss, w_rs, tz_ss, tp_ss, t_rs, td_ss, td_rs, pp_ss, pp_rs, p_ss, p_rs, pair_ss, pair_rs,
     mg_ss, mg_rs, g_ss, g_rs, row_ss, row_rs, col_ss, col_rs, st_ss, st_rs,
 ):
-    R, C, X, Z, T, Db, Dp, Fb, chunk, K = sizes
+    R, C, X, Z, T, Db, Dp, Fb, chunk, K, F2, F2p, Fw = sizes
     L = LOW
     plane = R * L
     devices = R * C
@@ -63,7 +63,7 @@
 
     lax.fori_loop(1, devices, greet, 0)
 
-    def send(src, dst, ss, rs, device, cond=None):
+    def send(src, dst, ss, rs, device, cond=None, bulk=False):
         def make():
             return pltpu.make_async_remote_copy(
                 src_ref=src, dst_ref=dst, send_sem=ss, recv_sem=rs,
@@ -72,10 +72,17 @@
 
         if cond is None:
             make().start()
+        else:
+            pl.when(cond)(lambda: make().start())
+        if bulk:
+            return
+        if cond is None:
             finish.append(lambda: make().wait_send())
         else:
-            pl.when(cond)(lambda: make().start())
             finish.append(lambda: pl.when(cond)(lambda: make().wait_send()))
+
+    def sent(like, ss):
+        finish.append(lambda: pltpu.make_async_copy(like, like, ss).wait())
 
     def arrived(slot, rs):
         pltpu.make_async_copy(slot, slot, rs).wait()
@@ -100,6 +107,8 @@
         txa[:, rows(own_slot, T), :] = jnp.zeros((L, T, Z * Dp), BF16)
         pool[...] = jnp.zeros(pool.shape, F32)
     wg[pl.ds(pl.multiple_of(z * Dp, Dp), Db)] = wv[...].astype(BF16)
+    if F2p != F2:
+        wg[F2:F2p] = jnp.zeros((F2p - F2, Fb), BF16)
     loads[1].wait()
     for k in range(R):
         hs[k] = hv[:, k * Fb:(k + 1) * Fb]
@@ -115,7 +124,8 @@
     pl.semaphore_wait(barrier, devices - 1)
     for o in range(1, plane):
         _, r2, y2 = plane_peer(o)
-        send(hs.at[r2], hid.at[rows(q, T)], hid_ss.at[o], hid_rs.at[q], (r2, z * L + y2))
+        send(hs.at[r2], hid.at[rows(q, T)], hid_ss, hid_rs, (r2, z * L + y2), bulk=True)
+    sent(hid.at[pl.ds(0, (plane - 1) * T)], hid_ss)
 
     def text_place(zs):
         return x * C + zs * L + y
@@ -141,13 +151,13 @@
                 h = 0 if n < X - 1 else 1
                 half = txa.at[h, rows(place, T), :]
                 onward = neighbours()[X - 1:] if h == 0 else neighbours()[:X - 1]
-                for m, (x3, y3) in enumerate(onward):
+                for x3, y3 in onward:
                     send(
-                        half, half, td_ss.at[d, s, n, m], td_rs.at[place, h],
-                        (x3 * CORES + core, z * L + y3), has if s else None,
+                        half, half, td_ss, td_rs,
+                        (x3 * CORES + core, z * L + y3), has if s else None, True,
                     )
 
-    for s in range(Z):
+    def texts_on(s):
         for d, direction in enumerate((1, -1)):
             zs = z - direction * s
             nz = z + direction
@@ -159,11 +169,13 @@
                 pl.when(has)(lambda: arrived(at, t_rs.at[place]))
             send(at, at, tz_ss.at[d, s], t_rs.at[place], (r, jnp.clip(nz, 0, Z - 1) * L + y), go)
             if s or d == 0:
-                for n, (x2, y2) in enumerate(neighbours()):
+                for x2, y2 in neighbours():
                     send(
-                        at, at, tp_ss.at[d, s, n], t_rs.at[place],
-                        (x2 * CORES + core, z * L + y2), has if s else None,
+                        at, at, tp_ss, t_rs.at[place],
+                        (x2 * CORES + core, z * L + y2), has if s else None, True,
                     )
+
+    def weights_on(s):
         for d, direction in enumerate((1, -1)):
             zs = z - direction * s
             nz = z + direction
@@ -173,59 +185,87 @@
             at = wg.at[rows(block, Dp)]
             if s:
                 pl.when(has)(lambda: arrived(at, w_rs.at[block]))
+            send(at, at, w_ss.at[d, s], w_rs.at[block], (r, jnp.clip(nz, 0, Z - 1) * L + y), go)
+
+    texts_on(0)
+    weights_on(0)
+    loads[3].wait()
+
+    def put_pool(h, at, value):
+        pool[h, :, at:at + Db] = value
+
+    by_half(pv[...].astype(F32), put_pool)
+    loads[4].wait()
+    loads[5].wait()
+    eye = lax.broadcasted_iota(jnp.int32, (Db, Db), 0) == lax.broadcasted_iota(jnp.int32, (Db, Db), 1)
+    line = jnp.broadcast_to(rmv[...].reshape(1, Db), (Db, Db))
+    rmc[...] = jnp.sum(jnp.where(eye, line, 0.0), axis=1, keepdims=True)
+    partner = (x * CORES + (1 - core), c)
+    low = z < Z // 2
+    spans = (
+        (pl.multiple_of(jnp.where(low, 0, Fw), 128), F2p - Fw),
+        (pl.multiple_of(jnp.where(low, F2p - Fw, 0), 128), Fw),
+    )
+
+    def project(g):
+        start, width = spans[g]
+        lanes = pl.ds(start, width)
+        part[:, lanes] = dot_nt(hid[...], wg[lanes])
+        for o in range(1, X + 1):
+            x2 = lax.rem(x + o, X)
             send(
-                at, at, w_ss.at[d, s], w_rs.at[block],
-                (r, jnp.clip(nz, 0, Z - 1) * L + y), go,
+                part.at[rows(x2 * CORES + 1 - core, L * T), lanes], pre.at[x2, :, lanes],
+                pp_ss, pp_rs.at[x2, g], partner, bulk=True,
             )
-        if s:
-            relay(s - 1)
+
+    def spread(g):
+        start, width = spans[g]
+        lanes = pl.ds(start, width)
+        for o in range(1, X + 1):
+            x2 = lax.rem(x + o, X)
+            arrived(pre.at[x2, :, lanes], pp_rs.at[x2, g])
+            summed[x2, :, lanes] = part[rows(x2 * CORES + core, L * T), lanes] + pre[x2, :, lanes]
+            for k in range(L):
+                y2 = lax.rem(y + 1 + k, L)
+                if o == X and k == L - 1:
+                    proj[x, y, :, lanes] = summed[x, rows(y, T), lanes]
+                else:
+                    send(
+                        summed.at[x2, rows(y2, T), lanes], proj.at[x, y, :, lanes], p_ss,
+                        p_rs.at[g], (x2 * CORES + core, z * L + y2), bulk=True,
+                    )
+
+    def gathered(g):
+        start, width = spans[g]
+        arrived(part.at[pl.ds(0, (X * L - 1) * T), pl.ds(start, width)], p_rs.at[g])
+
+    for s in range(1, Z):
+        texts_on(s)
+        if s == Z - 1:
+            spread(0)
         else:
-            loads[3].wait()
-
-            def put_pool(h, at, value):
-                pool[h, :, at:at + Db] = value
-
-            by_half(pv[...].astype(F32), put_pool)
-            loads[4].wait()
-            loads[5].wait()
-            eye = lax.broadcasted_iota(jnp.int32, (Db, Db), 0) == lax.broadcasted_iota(jnp.int32, (Db, Db), 1)
-            line = jnp.broadcast_to(rmv[...].reshape(1, Db), (Db, Db))
-            rmc[...] = jnp.sum(jnp.where(eye, line, 0.0), axis=1, keepdims=True)
-    for o in range(1, plane):
-        other, _, _ = plane_peer(o)
-        arrived(hid.at[rows(other, T)], hid_rs.at[other])
-
-    part[...] = dot_nt(hid[...], wg[...])
-    partner = (x * CORES + (1 - core), c)
-    for o in range(1, X + 1):
-        x2 = lax.rem(x + o, X)
-        send(
-            part.at[rows(x2 * CORES + 1 - core, L * T)], pre.at[x2],
-            pp_ss.at[o], pp_rs.at[x2], partner,
-        )
+            weights_on(s)
+        relay(s - 1)
+        if s == Z - 2:
+            arrived(hid.at[pl.ds(0, (plane - 1) * T)], hid_rs)
+            project(0)
+    weights_on(Z - 1)
+    project(1)
+    count = (X - 1) * (L - 1) * Z * T
+    sent(txa.at[:, pl.ds(0, count), :], td_ss)
+    sent(txa.at[:, pl.ds(0, Z * (X + L - 2) * T), :], tp_ss)
+    sent(part.at[pl.ds(0, X * L * T)], pp_ss)
+    sent(part.at[pl.ds(0, (X * L - 1) * T)], p_ss)
     relay(Z - 1)
-    for o in range(1, X + 1):
-        x2 = lax.rem(x + o, X)
-        arrived(pre.at[x2], pp_rs.at[x2])
-        summed[x2] = part[rows(x2 * CORES + core, L * T)] + pre[x2]
-        for k in range(L):
-            y2 = lax.rem(y + 1 + k, L)
-            if o == X and k == L - 1:
-                proj[x, y] = summed[x, rows(y, T)]
-            else:
-                send(
-                    summed.at[x2, rows(y2, T)], proj.at[x, y], p_ss.at[o * L + k],
-                    p_rs.at[x * L + y], (x2 * CORES + core, z * L + y2),
-                )
-    for o in range(1, X * L):
-        other = lax.rem(x * L + y + o, X * L)
-        arrived(proj.at[other // L, other % L], p_rs.at[other])
+    spread(1)
+    gathered(0)
+    gathered(1)
     mixed = []
     for h in range(L):
         total = proj[0, h]
         for k in range(1, X):
             total = total + proj[k, h]
-        mixed.append(pool[h] + total)
+        mixed.append(pool[h] + total[:, :F2])
     square = sum(jnp.sum(m * m, axis=1, keepdims=True) for m in mixed)
     length = jnp.sqrt(square + EPSILON)
     unit = [m / length for m in mixed]
@@ -233,12 +273,7 @@
         img_s[h] = unit[h].astype(BF16)
     send(img_s, img_r, pair_ss.at[0], pair_rs.at[0], partner)
 
-    for ox in range(1, X):
-        for oy in range(1, L):
-            for zs in range(Z):
-                place = lax.rem(x + ox, X) * C + zs * L + lax.rem(y + oy, L)
-                for h in range(L):
-                    arrived(txa.at[h, rows(place, T), :], td_rs.at[place, h])
+    arrived(txa.at[:, pl.ds(0, count), :], td_rs)
 
     scale = jnp.exp(jnp.full((1, 1), ls_ref[0], F32))
     bias = jnp.full((1, 1), bias_ref[0], F32)
@@ -284,23 +319,25 @@
     inner = sum(jnp.sum(unit[h] * ug[h], axis=1, keepdims=True) for h in range(L))
     for h in range(L):
         mg_s[h] = ((ug[h] - unit[h] * inner) / length).astype(BF16)
-    for o in range(1, X * L):
-        other = lax.rem(x * L + y + o, X * L)
+    others = [
+        (lax.rem(x + ox, X), lax.rem(y + oy, L))
+        for ox in reversed(range(X)) for oy in reversed(range(L)) if ox or oy
+    ]
+    for x2, y2 in others:
         send(
-            mg_s.at[other % L], mga.at[rows(q, T)], mg_ss.at[o], mg_rs.at[q],
-            ((other // L) * CORES + core, z * L + other % L),
+            mg_s.at[y2], mga.at[rows(q, T)], mg_ss, mg_rs.at[q],
+            (x2 * CORES + core, z * L + y2), bulk=True,
         )
-    send(mg_s.at[y], mga.at[rows(q, T)], mg_ss.at[0], mg_rs.at[q], partner)
+    send(mg_s.at[y], mga.at[rows(q, T)], mg_ss, mg_rs.at[q], partner, bulk=True)
     mga[rows(q, T)] = mg_s[y]
-    for o in range(1, X * L):
-        other = lax.rem(x * L + y + o, X * L)
-        source = ((other // L) * CORES + core) * L + other % L
+    for x2, y2 in others:
+        source = (x2 * CORES + core) * L + y2
         at = mga.at[rows(source, T)]
         arrived(at, mg_rs.at[source])
-        send(at, at, mg_ss.at[X * L + o], mg_rs.at[source], partner)
-    for o in range(X * L):
-        other = lax.rem(x * L + y + o, X * L)
-        source = ((other // L) * CORES + 1 - core) * L + other % L
+        send(at, at, mg_ss, mg_rs.at[source], partner, bulk=True)
+    sent(mga.at[pl.ds(0, (plane - 1) * T)], mg_ss)
+    for x2, y2 in [(x, y)] + others:
+        source = (x2 * CORES + 1 - core) * L + y2
         arrived(mga.at[rows(source, T)], mg_rs.at[source])
 
     turned[...] = mga[...].T
@@ -319,7 +356,7 @@
         cut = rows(k, Dc)
         copy = pltpu.make_async_remote_copy(
             src_ref=gz_s.at[zd, cut], dst_ref=gz.at[d, zd, cut],
-            send_sem=g_ss.at[d, zd, k], recv_sem=g_rs.at[d, zd, k],
+            send_sem=g_ss, recv_sem=g_rs.at[d, zd, k],
             device_id=(r, jnp.clip(z + (1 if d == 0 else -1), 0, Z - 1) * L + y), device_id_type=MESH,
         )
         return place, zd, k, cut, jnp.logical_and(ready, beyond), jnp.logical_and(ready, zd == z), copy
@@ -347,12 +384,6 @@
             pl.when(jnp.logical_and(ending, place > 0))(last)
         return _
 
-    def drain(tau, _):
-        for d in range(2):
-            passing, copy = pieces(tau, d)[4::2]
-            pl.when(passing)(lambda: copy.wait_send())
-        return _
-
     steps_g = max((Z - 1) * K + 1, K - 1 + 2 * (Z - 1)) + 1
     head = min(K, 2)
 
@@ -363,6 +394,7 @@
     lax.fori_loop(0, head, step, 0)
     for k in range(1, Z):
         own_part(order(k))
+    sent(gz_s.at[pl.ds(0, Z - 1)], g_ss)
     lax.fori_loop(head, steps_g, step, 0)
     g = gp[z][:Db]
 
@@ -371,16 +403,14 @@
     csb[c] = jnp.sum(sq, axis=0, keepdims=True)
     for o in range(1, C):
         c2 = lax.rem(c + o, C)
-        send(csb.at[c], csb.at[c], col_ss.at[o], col_rs.at[c], (r, c2))
+        send(csb.at[c], csb.at[c], col_ss, col_rs, (r, c2), bulk=True)
     for o in range(1, R):
         r2 = lax.rem(r + o, R)
-        send(rsb.at[r], rsb.at[r], row_ss.at[o], row_rs.at[r], (r2, c))
-    for o in range(1, R):
-        r2 = lax.rem(r + o, R)
-        arrived(rsb.at[r2], row_rs.at[r2])
-    for o in range(1, C):
-        c2 = lax.rem(c + o, C)
-        arrived(csb.at[c2], col_rs.at[c2])
+        send(rsb.at[r], rsb.at[r], row_ss, row_rs, (r2, c), bulk=True)
+    sent(csb.at[pl.ds(0, C - 1)], col_ss)
+    sent(rsb.at[pl.ds(0, R - 1)], row_ss)
+    arrived(rsb.at[pl.ds(0, R - 1)], row_rs)
+    arrived(csb.at[pl.ds(0, C - 1)], col_rs)
     row_sum = sum(rsb[k] for k in range(R))
     col_sum = sum(csb[k] for k in range(C))
     new_row = DECAY_RATE * rmc[...] + (1.0 - DECAY_RATE) * row_sum / (R * Fb)
@@ -394,33 +424,21 @@
     lane = lax.broadcasted_iota(jnp.int32, (1, 128), 1)
     stb[me] = jnp.where(lane == 0, local, loss_local)
 
-    def tell(o, wait):
+    def tell(o, _):
         other = lax.rem(me + o, devices)
-        copy = pltpu.make_async_remote_copy(
-            src_ref=stb.at[me], dst_ref=stb.at[me], send_sem=st_ss.at[o], recv_sem=st_rs.at[me],
+        pltpu.make_async_remote_copy(
+            src_ref=stb.at[me], dst_ref=stb.at[me], send_sem=st_ss, recv_sem=st_rs,
             device_id=(other // C, other % C), device_id_type=MESH,
-        )
-        if wait:
-            copy.wait_send()
-            arrived(stb.at[other], st_rs.at[other])
-        else:
-            copy.start()
-
-    def tell_start(o, _):
-        tell(o, False)
+        ).start()
         return _
 
-    def tell_wait(o, _):
-        tell(o, True)
-        return _
-
-    lax.fori_loop(1, devices, tell_start, 0)
-    lax.fori_loop(1, devices, tell_wait, 0)
+    lax.fori_loop(1, devices, tell, 0)
+    sent(stb.at[pl.ds(0, devices - 1)], st_ss)
+    arrived(stb.at[pl.ds(0, devices - 1)], st_rs)
     totals = jnp.sum(stb[...], axis=0)
     rms = jnp.sqrt(totals[:, 0:1] / (C * Db * R * Fb))
     upd_ref[...] = upd_ref[...] / jnp.maximum(1.0, rms / CLIP_LEVEL)
     loss_ref[0] = jnp.sum(jnp.where(lane == 1, totals, 0.0)) / batch
-    lax.fori_loop(0, steps_g, drain, 0)
     for wait in finish:
         wait()
 
@@ -437,10 +455,13 @@
     chunk = min(texts, 512)
 
     K = 3 if Dp % 48 == 0 else 1
-    sizes = (R, C, X, Z, T, Db, Dp, Fb, chunk, K)
+    F2p = -(-F2 // 128) * 128
+    Fw = max(-(-Dp // 128) * 128, F2p - (F2 - Dp) // 128 * 128)
+    sizes = (R, C, X, Z, T, Db, Dp, Fb, chunk, K, F2, F2p, Fw)
     vmem = pl.BlockSpec(memory_space=pltpu.VMEM)
     smem = pl.BlockSpec(memory_space=pltpu.SMEM)
     dma = lambda *s: pltpu.SemaphoreType.DMA(s)
+    one = pltpu.SemaphoreType.DMA
     upd, nr, nc, loss = pl.pallas_call(
         functools.partial(kernel, sizes),
         out_shape=(
@@ -462,12 +483,12 @@
             pltpu.VMEM((L, T, F2), F32),
             pltpu.VMEM((Db, 1), F32),
             pltpu.VMEM((plane * T, Fb), BF16),
-            pltpu.VMEM((F2, Fb), BF16),
+            pltpu.VMEM((F2p, Fb), BF16),
             pltpu.VMEM((L, texts, F2), BF16),
-            pltpu.VMEM((plane * T, F2), F32),
-            pltpu.VMEM((X, L * T, F2), F32),
-            pltpu.VMEM((X, L * T, F2), F32),
-            pltpu.VMEM((X, L, T, F2), F32),
+            pltpu.VMEM((plane * T, F2p), F32),
+            pltpu.VMEM((X, L * T, F2p), F32),
+            pltpu.VMEM((X, L * T, F2p), F32),
+            pltpu.VMEM((X, L, T, F2p), F32),
             pltpu.VMEM((L, T, F2), BF16),
             pltpu.VMEM((L, T, F2), BF16),
             pltpu.VMEM((L, T, F2), F32),
@@ -482,10 +503,9 @@
             pltpu.VMEM((C, 1, Fb), F32),
             pltpu.VMEM((R * C, 1, 128), F32),
             dma(6),
-            dma(plane), dma(plane), dma(2, Z), dma(Z), dma(2, Z), dma(2, Z, X + L), dma(X * C),
-            dma(2, Z, X + L, X + L), dma(X * C, L), dma(X + 1), dma(X), dma(X * L + L), dma(X * L),
-            dma(2), dma(2), dma(plane), dma(plane), dma(2, Z, K), dma(2, Z, K),
-            dma(R), dma(R), dma(C), dma(C), dma(R * C), dma(R * C),
+            one, one, dma(2, Z), dma(Z), dma(2, Z), one, dma(X * C), one, one,
+            one, dma(X, 2), one, dma(2), dma(2), dma(2),
+            one, dma(plane), one, dma(2, Z, K), one, one, one, one, one, one,
         ],
         compiler_params=pltpu.CompilerParams(
             has_side_effects=True, collective_id=0, vmem_limit_bytes=60 * 1024 * 1024

time: 111 us -> 104 us (0.937)
  Pallas kernels: 104 us -> 97 us
    pallas_call x1, Pallas kernels: 104 us -> 97 us  [per_device(): pl.pallas_call(functools.partial(kernel, sizes), out_shape=(jax.ShapeDtyp...]
where the time goes in v2:
time: 104 us
  Pallas kernels  97 us (93%)
  between operations  3.75 us (4%)
  local copies, waits for them, and re-layouts  3.15 us (3%)
    pallas_call x1, Pallas kernels, per_device(): pl.pallas_call(functools.partial(kernel, sizes), out_shape=(jax.ShapeDtyp...  97 us
    unnamed x7, local copies, waits for them, and re-layouts  3.15 us

profile of v2, /device:TPU:0, one launch (start us, length us, event | category | flops | bytes accessed | tf_op | source)
XLA Modules:
  0.0 103.9 jit_solution(1310710751170903497)
XLA Ops:
  1.9 97.0 %shard_map.111 = (f32[144,1076]{1,0:T(8,128)}, f32[144]{0:T(256)}, f32[1076]{0:T(1024)}, f32[1]{0:T(128)}) custom-call(bf16[64,4304]{1,0:T(8,128)(2,1)} %hid_in.1, f32[144,1076]{1,0:T(8,128)} %w_in.1, bf16[64,1152]{1,0:T(8,128)(2,1)} %pool_in.1, bf16[64,1152]{1,0:T(8,128)(2,1)} %text_in.1, f32[144]{0:T(256)} %rm_in.1, f32[1076]{0:T(1024)} %cm_in.1, ...), custom_call_target="tpu_custom_call" | custom-call | tf_op jit(solution)/shard_map/pallas_call | solution.py:465
  98.9 0.0 copy-start.1
  98.9 0.0 copy-start
  98.9 2.0 %copy.18 = f32[144,1076]{1,0:T(8,128)} copy(f32[144,1076]{1,0:T(8,128)} %get-tuple-element.16) | data formatting | bytes 1239552
  100.9 0.0 copy-done.1
  100.9 0.6 copy.19
  101.5 0.0 copy-done
  101.5 0.6 copy.20
Async XLA Ops:
  98.9 2.0 %copy-start.1 = (f32[144]{0:T(256)S(1)}, f32[144]{0:T(256)}, u32[]{:S(2)}) copy-start(f32[144]{0:T(256)} %get-tuple-element.17) | copy-start | bytes 1732
  98.9 2.6 %copy-start = (f32[1076]{0:T(1024)S(1)}, f32[1076]{0:T(1024)}, u32[]{:S(2)}) copy-start(f32[1076]{0:T(1024)} %get-tuple-element.18) | copy-start | bytes 12916

commit v3 on v2

--- a/solution.py
+++ b/solution.py
@@ -27,12 +27,12 @@
     hid_in, w_in, pool_in, text_in, rm_in, cm_in, ls_ref, bias_ref,
     upd_ref, nr_ref, nc_ref, loss_ref,
     hv, wv, pv, tv, rmv, cmv, hs, pool, rmc,
-    hid, wg, txa, part, pre, summed, proj, img_s, img_r, ug_s, ug_r, mg_s, mga, turned, gp, gz_s, gz,
+    hid, wg, txa, part, pre, summed, proj, mix, imgs, ug_s, ug_r, mg_s, mga, turned, gp, gz_s, gz,
     rsb, csb, stb, ld,
-    hid_ss, hid_rs, w_ss, w_rs, tz_ss, tp_ss, t_rs, td_ss, td_rs, pp_ss, pp_rs, p_ss, p_rs, pair_ss, pair_rs,
+    hid_ss, hid_rs, hx_rs, w_ss, w_rs, tz_ss, tp_ss, t_rs, td_ss, td_rs, pp_ss, pp_rs, p_ss, p_rs, pair_ss, pair_rs,
     mg_ss, mg_rs, g_ss, g_rs, row_ss, row_rs, col_ss, col_rs, st_ss, st_rs,
 ):
-    R, C, X, Z, T, Db, Dp, Fb, chunk, K, F2, F2p, Fw = sizes
+    R, C, X, Z, T, Db, Dp, Fb, K, F2, F2p, Fw = sizes
     L = LOW
     plane = R * L
     devices = R * C
@@ -56,12 +56,14 @@
         load.start()
     barrier = pltpu.get_barrier_semaphore()
 
-    def greet(o, _):
-        other = lax.rem(me + o, devices)
-        pl.semaphore_signal(barrier, inc=1, device_id=(other // C, other % C), device_id_type=MESH)
-        return _
-
-    lax.fori_loop(1, devices, greet, 0)
+    def greet(device):
+        pl.semaphore_signal(barrier, inc=1, device_id=device, device_id_type=MESH)
+
+    for o in range(1, plane):
+        other = lax.rem(q + o, plane)
+        greet((other // L, z * L + other % L))
+    pl.when(z > 0)(lambda: greet((r, c - L)))
+    pl.when(z < Z - 1)(lambda: greet((r, c + L)))
 
     def send(src, dst, ss, rs, device, cond=None, bulk=False):
         def make():
@@ -87,10 +89,6 @@
     def arrived(slot, rs):
         pltpu.make_async_copy(slot, slot, rs).wait()
 
-    def plane_peer(o):
-        other = lax.rem(q + o, plane)
-        return other, other // L, other % L
-
     def rows(index, count):
         return pl.ds(pl.multiple_of(index * count, count), count)
 
@@ -98,13 +96,13 @@
         for h in range(L):
             for k in range(Z):
                 at = (k * L + h) * Db
-                store(h, k * Dp, value[:, at:at + Db])
-
-    own_slot = x * C + c
+                store(h * F2 + k * Dp, value[:, at:at + Db])
+
+    own_slot = (z * X + x) * L + y
     loads[0].wait()
     if Dp != Db:
         wg[rows(z, Dp)] = jnp.zeros((Dp, Fb), BF16)
-        txa[:, rows(own_slot, T), :] = jnp.zeros((L, T, Z * Dp), BF16)
+        txa[rows(own_slot, T)] = jnp.zeros((T, L * F2), BF16)
         pool[...] = jnp.zeros(pool.shape, F32)
     wg[pl.ds(pl.multiple_of(z * Dp, Dp), Db)] = wv[...].astype(BF16)
     if F2p != F2:
@@ -117,22 +115,47 @@
     tf = tv[...].astype(F32)
     tn = tf / jnp.sqrt(jnp.sum(tf * tf, axis=1, keepdims=True) + EPSILON)
 
-    def put_text(h, at, value):
-        txa[h, rows(own_slot, T), at:at + Db] = value.astype(BF16)
+    def put_text(at, value):
+        txa[rows(own_slot, T), at:at + Db] = value.astype(BF16)
 
     by_half(tn, put_text)
-    pl.semaphore_wait(barrier, devices - 1)
-    for o in range(1, plane):
-        _, r2, y2 = plane_peer(o)
-        send(hs.at[r2], hid.at[rows(q, T)], hid_ss, hid_rs, (r2, z * L + y2), bulk=True)
-    sent(hid.at[pl.ds(0, (plane - 1) * T)], hid_ss)
+    pl.semaphore_wait(barrier, plane - 1 + jnp.where(z > 0, 1, 0) + jnp.where(z < Z - 1, 1, 0))
+    across = [lax.rem(x + o, X) for o in range(1, X)]
+    beside = [lax.rem(y + o, L) for o in range(1, L)]
+    partner = (x * CORES + (1 - core), c)
+    own_rows = hid.at[rows(q, T)]
+    for x2 in across:
+        for k in range(CORES):
+            r2 = x2 * CORES + k
+            send(hs.at[r2], own_rows, hid_ss, hx_rs, (r2, c), bulk=True)
+    for y2 in beside:
+        for k in range(CORES):
+            r2 = x * CORES + k
+            send(hs.at[r2], own_rows, hid_ss, hid_rs, (r2, z * L + y2), bulk=True)
+    send(hs.at[partner[0]], own_rows, hid_ss, hid_rs, partner, bulk=True)
+    crossing = (X - 1) * CORES
+    relayed = crossing * (L - 1)
+    direct = crossing + CORES * (L - 1) + 1
+
+    def hidden_on():
+        arrived(hid.at[pl.ds(0, crossing * T)], hx_rs)
+        for x2 in across:
+            for k in range(CORES):
+                at = hid.at[rows((x2 * CORES + k) * L + y, T)]
+                for y2 in beside:
+                    send(at, at, hid_ss, hid_rs, (r, z * L + y2), bulk=True)
+        sent(hid.at[pl.ds(0, (direct + relayed) * T)], hid_ss)
 
     def text_place(zs):
-        return x * C + zs * L + y
+        return (zs * X + x) * L + y
 
     def neighbours():
         along_x = [(lax.rem(x + o, X), y) for o in range(1, X)]
         return along_x + [(x, lax.rem(y + o, L)) for o in range(1, L)]
+
+    split = T // 4
+    low = z < Z // 2
+    final = jnp.where(low, Z - 1, 0)
 
     def relay(s):
         for d, direction in enumerate((1, -1)):
@@ -142,18 +165,19 @@
             has = jnp.logical_and(zs >= 0, zs < Z)
             block = jnp.clip(zs, 0, Z - 1)
             for n, (x2, y2) in enumerate(neighbours()):
-                place = x2 * C + block * L + y2
-                at = txa.at[:, rows(place, T), :]
+                place = (block * X + x2) * L + y2
+                at = txa.at[rows(place, T)]
                 if s:
                     pl.when(has)(lambda: arrived(at, t_rs.at[place]))
                 else:
                     arrived(at, t_rs.at[place])
                 h = 0 if n < X - 1 else 1
-                half = txa.at[h, rows(place, T), :]
+                part_at = pl.multiple_of(place * T + h * split, split)
+                half = txa.at[pl.ds(part_at, T - split if h else split)]
                 onward = neighbours()[X - 1:] if h == 0 else neighbours()[:X - 1]
                 for x3, y3 in onward:
                     send(
-                        half, half, td_ss, td_rs,
+                        half, half, td_ss, td_rs.at[jnp.where(block == final, 1, 0)],
                         (x3 * CORES + core, z * L + y3), has if s else None, True,
                     )
 
@@ -164,7 +188,7 @@
             has = jnp.logical_and(zs >= 0, zs < Z)
             go = jnp.logical_and(has, jnp.logical_and(nz >= 0, nz < Z))
             place = text_place(jnp.clip(zs, 0, Z - 1))
-            at = txa.at[:, rows(place, T), :]
+            at = txa.at[rows(place, T)]
             if s:
                 pl.when(has)(lambda: arrived(at, t_rs.at[place]))
             send(at, at, tz_ss.at[d, s], t_rs.at[place], (r, jnp.clip(nz, 0, Z - 1) * L + y), go)
@@ -191,8 +215,8 @@
     weights_on(0)
     loads[3].wait()
 
-    def put_pool(h, at, value):
-        pool[h, :, at:at + Db] = value
+    def put_pool(at, value):
+        pool[:, at:at + Db] = value
 
     by_half(pv[...].astype(F32), put_pool)
     loads[4].wait()
@@ -200,8 +224,6 @@
     eye = lax.broadcasted_iota(jnp.int32, (Db, Db), 0) == lax.broadcasted_iota(jnp.int32, (Db, Db), 1)
     line = jnp.broadcast_to(rmv[...].reshape(1, Db), (Db, Db))
     rmc[...] = jnp.sum(jnp.where(eye, line, 0.0), axis=1, keepdims=True)
-    partner = (x * CORES + (1 - core), c)
-    low = z < Z // 2
     spans = (
         (pl.multiple_of(jnp.where(low, 0, Fw), 128), F2p - Fw),
         (pl.multiple_of(jnp.where(low, F2p - Fw, 0), 128), Fw),
@@ -241,84 +263,80 @@
 
     for s in range(1, Z):
         texts_on(s)
+        if s == 1:
+            hidden_on()
         if s == Z - 1:
             spread(0)
         else:
             weights_on(s)
         relay(s - 1)
         if s == Z - 2:
-            arrived(hid.at[pl.ds(0, (plane - 1) * T)], hid_rs)
+            arrived(hid.at[pl.ds(0, (plane - 1 - crossing) * T)], hid_rs)
             project(0)
     weights_on(Z - 1)
     project(1)
-    count = (X - 1) * (L - 1) * Z * T
-    sent(txa.at[:, pl.ds(0, count), :], td_ss)
-    sent(txa.at[:, pl.ds(0, Z * (X + L - 2) * T), :], tp_ss)
     sent(part.at[pl.ds(0, X * L * T)], pp_ss)
     sent(part.at[pl.ds(0, (X * L - 1) * T)], p_ss)
     relay(Z - 1)
     spread(1)
+    pairs_each = (X - 1) * (L - 1) * T
+    sent(txa.at[pl.ds(0, Z * pairs_each)], td_ss)
+    sent(txa.at[pl.ds(0, Z * (X + L - 2) * T)], tp_ss)
     gathered(0)
     gathered(1)
-    mixed = []
     for h in range(L):
         total = proj[0, h]
         for k in range(1, X):
             total = total + proj[k, h]
-        mixed.append(pool[h] + total[:, :F2])
-    square = sum(jnp.sum(m * m, axis=1, keepdims=True) for m in mixed)
-    length = jnp.sqrt(square + EPSILON)
-    unit = [m / length for m in mixed]
-    for h in range(L):
-        img_s[h] = unit[h].astype(BF16)
-    send(img_s, img_r, pair_ss.at[0], pair_rs.at[0], partner)
-
-    arrived(txa.at[:, pl.ds(0, count), :], td_rs)
-
+        mix[:, h * F2:(h + 1) * F2] = total[:, :F2]
+    mixed = mix[...] + pool[...]
+    length = jnp.sqrt(jnp.sum(mixed * mixed, axis=1, keepdims=True) + EPSILON)
+    unit = mixed / length
+    imgs[:T] = unit.astype(BF16)
+    theirs = imgs.at[pl.ds(T, T)]
+    send(imgs.at[pl.ds(0, T)], theirs, pair_ss.at[0], pair_rs.at[0], partner)
     scale = jnp.exp(jnp.full((1, 1), ls_ref[0], F32))
     bias = jnp.full((1, 1), bias_ref[0], F32)
-    steps = X * C * T // chunk
-
-    def pairs(images, own):
-        halves = [images[h] for h in range(L)]
-
-        def step(i, carry):
-            loss, grads = carry
-            cut = pl.ds(pl.multiple_of(i * chunk, chunk), chunk)
-            texts = [txa[h, cut, :] for h in range(L)]
-            logits = scale * sum(dot_nt(halves[h], texts[h]) for h in range(L)) + bias
-            if own:
-                row_id = lax.broadcasted_iota(jnp.int32, logits.shape, 0) + own_slot * T
-                col_id = lax.broadcasted_iota(jnp.int32, logits.shape, 1) + i * chunk
-                sign = jnp.where(row_id == col_id, F32(1.0), F32(-1.0))
-            else:
-                sign = F32(-1.0)
-            u = -sign * logits
-            e = jnp.exp(-jnp.abs(u))
-            loss = loss + jnp.sum(jnp.maximum(u, 0.0) + jnp.log1p(e), axis=1, keepdims=True)
-            sig = jnp.where(u >= 0, F32(1.0), e) / (1.0 + e)
-            pg = (-sign * sig / batch).astype(BF16)
-            grads = tuple(
-                grads[h] + jnp.dot(pg, texts[h], preferred_element_type=F32) for h in range(L)
-            )
-            return loss, grads
-
-        zero = (jnp.zeros((T, 1), F32), tuple(jnp.zeros((T, Z * Dp), F32) for _ in range(L)))
-        if steps == 1:
-            return step(0, zero)
-        return lax.fori_loop(0, steps, step, zero)
-
-    arrived(img_r, pair_rs.at[0])
-    loss_b, grads_b = pairs(img_r, False)
+    width = X * L * T
+
+    def pairs(top, count, zs):
+        images = imgs[top:top + count]
+        texts = txa[rows(zs, width)]
+        logits = scale * dot_nt(images, texts) + bias
+        row_id = lax.broadcasted_iota(jnp.int32, logits.shape, 0) + top
+        col_id = lax.broadcasted_iota(jnp.int32, logits.shape, 1) + (zs * width - own_slot * T)
+        match = jnp.logical_and(row_id == col_id, row_id < T)
+        u = jnp.where(match, -logits, logits)
+        e = jnp.exp(-jnp.abs(u))
+        loss = jnp.sum(jnp.maximum(u, 0.0) + jnp.log1p(e), axis=1, keepdims=True)
+        sig = jnp.where(u >= 0, F32(1.0), e) / (1.0 + e)
+        pg = (jnp.where(match, -sig, sig) / batch).astype(BF16)
+        return loss, jnp.dot(pg, texts, preferred_element_type=F32)
+
+    def more(k, carry):
+        loss, grads = pairs(0, 2 * T, jnp.where(low, k, Z - 1 - k))
+        return carry[0] + loss, carry[1] + grads
+
+    arrived(txa.at[pl.ds(0, (Z - 1) * pairs_each)], td_rs.at[0])
+    arrived(theirs, pair_rs.at[0])
+    carry = (jnp.zeros((2 * T, 1), F32), jnp.zeros((2 * T, L * F2), F32))
+    if Z <= 4:
+        for k in range(Z - 1):
+            carry = more(k, carry)
+    else:
+        carry = lax.fori_loop(0, Z - 1, more, carry)
+    loss_most, grads = carry
+    arrived(txa.at[pl.ds(0, pairs_each)], td_rs.at[1])
+    loss_b, grads_b = pairs(T, T, final)
+    ug_s[...] = scale * (grads[T:] + grads_b)
+    send(ug_s, ug_r, pair_ss.at[1], pair_rs.at[1], partner)
+    loss_a, grads_a = pairs(0, T, final)
+    arrived(ug_r, pair_rs.at[1])
+    ug = scale * (grads[:T] + grads_a) + ug_r[...]
+    inner = jnp.sum(unit * ug, axis=1, keepdims=True)
+    mg = ((ug - unit * inner) / length).astype(BF16)
     for h in range(L):
-        ug_s[h] = scale * grads_b[h]
-    send(ug_s, ug_r, pair_ss.at[1], pair_rs.at[1], partner)
-    loss_a, grads_a = pairs(img_s, True)
-    arrived(ug_r, pair_rs.at[1])
-    ug = [scale * grads_a[h] + ug_r[h] for h in range(L)]
-    inner = sum(jnp.sum(unit[h] * ug[h], axis=1, keepdims=True) for h in range(L))
-    for h in range(L):
-        mg_s[h] = ((ug[h] - unit[h] * inner) / length).astype(BF16)
+        mg_s[h] = mg[:, h * F2:(h + 1) * F2]
     others = [
         (lax.rem(x + ox, X), lax.rem(y + oy, L))
         for ox in reversed(range(X)) for oy in reversed(range(L)) if ox or oy
@@ -420,7 +438,7 @@
     raw = g / jnp.sqrt(new_row * new_col)
     upd_ref[...] = raw
     local = jnp.sum(jnp.sum(raw * raw, axis=1, keepdims=True), axis=0, keepdims=True)
-    loss_local = jnp.sum(loss_a + loss_b, axis=0, keepdims=True)
+    loss_local = jnp.sum(loss_a + loss_b, axis=0, keepdims=True) + jnp.sum(loss_most, axis=0, keepdims=True)
     lane = lax.broadcasted_iota(jnp.int32, (1, 128), 1)
     stb[me] = jnp.where(lane == 0, local, loss_local)
 
@@ -452,12 +470,11 @@
     F2 = Z * Dp
     plane = R * L
     texts = X * C * T
-    chunk = min(texts, 512)
 
     K = 3 if Dp % 48 == 0 else 1
     F2p = -(-F2 // 128) * 128
     Fw = max(-(-Dp // 128) * 128, F2p - (F2 - Dp) // 128 * 128)
-    sizes = (R, C, X, Z, T, Db, Dp, Fb, chunk, K, F2, F2p, Fw)
+    sizes = (R, C, X, Z, T, Db, Dp, Fb, K, F2, F2p, Fw)
     vmem = pl.BlockSpec(memory_space=pltpu.VMEM)
     smem = pl.BlockSpec(memory_space=pltpu.SMEM)
     dma = lambda *s: pltpu.SemaphoreType.DMA(s)
@@ -480,19 +497,19 @@
             pltpu.VMEM((Db,), F32),
             pltpu.VMEM((Fb,), F32),
             pltpu.VMEM((R, T, Fb), BF16),
-            pltpu.VMEM((L, T, F2), F32),
+            pltpu.VMEM((T, L * F2), F32),
             pltpu.VMEM((Db, 1), F32),
             pltpu.VMEM((plane * T, Fb), BF16),
             pltpu.VMEM((F2p, Fb), BF16),
-            pltpu.VMEM((L, texts, F2), BF16),
+            pltpu.VMEM((texts, L * F2), BF16),
             pltpu.VMEM((plane * T, F2p), F32),
             pltpu.VMEM((X, L * T, F2p), F32),
             pltpu.VMEM((X, L * T, F2p), F32),
             pltpu.VMEM((X, L, T, F2p), F32),
-            pltpu.VMEM((L, T, F2), BF16),
-            pltpu.VMEM((L, T, F2), BF16),
-            pltpu.VMEM((L, T, F2), F32),
-            pltpu.VMEM((L, T, F2), F32),
+            pltpu.VMEM((T, L * F2), F32),
+            pltpu.VMEM((2 * T, L * F2), BF16),
+            pltpu.VMEM((T, L * F2), F32),
+            pltpu.VMEM((T, L * F2), F32),
             pltpu.VMEM((L, T, F2), BF16),
             pltpu.VMEM((plane * T, F2), BF16),
             pltpu.VMEM((F2, plane * T), BF16),
@@ -503,7 +520,7 @@
             pltpu.VMEM((C, 1, Fb), F32),
             pltpu.VMEM((R * C, 1, 128), F32),
             dma(6),
-            one, one, dma(2, Z), dma(Z), dma(2, Z), one, dma(X * C), one, one,
+            one, one, one, dma(2, Z), dma(Z), dma(2, Z), one, dma(X * C), one, dma(2),
             one, dma(X, 2), one, dma(2), dma(2), dma(2),
             one, dma(plane), one, dma(2, Z, K), one, one, one, one, one, one,
         ],

time: 104 us -> 101 us (0.971)
  Pallas kernels: 97 us -> 93.5 us
    pallas_call x1, Pallas kernels: 97 us -> 93.5 us  [per_device(): pl.pallas_call(functools.partial(kernel, sizes), out_shape=(jax.ShapeDtyp...]
where the time goes in v3:
time: 101 us; the launch traced here: 100 us
  Pallas kernels  93.5 us (93%)
  between operations  3.75 us (4%)
  local copies, waits for them, and re-layouts  3.15 us (3%)
    pallas_call x1, Pallas kernels, per_device(): pl.pallas_call(functools.partial(kernel, sizes), out_shape=(jax.ShapeDtyp...  93.5 us
    unnamed x7, local copies, waits for them, and re-layouts  3.15 us

profile of v3, /device:TPU:0, one launch (start us, length us, event | category | flops | bytes accessed | tf_op | source)
XLA Modules:
  0.0 100.4 jit_solution(15138459716359880776)
XLA Ops:
  1.9 93.5 %shard_map.111 = (f32[144,1076]{1,0:T(8,128)}, f32[144]{0:T(256)}, f32[1076]{0:T(1024)}, f32[1]{0:T(128)}) custom-call(bf16[64,4304]{1,0:T(8,128)(2,1)} %hid_in.1, f32[144,1076]{1,0:T(8,128)} %w_in.1, bf16[64,1152]{1,0:T(8,128)(2,1)} %pool_in.1, bf16[64,1152]{1,0:T(8,128)(2,1)} %text_in.1, f32[144]{0:T(256)} %rm_in.1, f32[1076]{0:T(1024)} %cm_in.1, ...), custom_call_target="tpu_custom_call" | custom-call | tf_op jit(solution)/shard_map/pallas_call | solution.py:482
  95.4 0.0 copy-start.1
  95.5 0.0 copy-start
  95.5 2.0 %copy.18 = f32[144,1076]{1,0:T(8,128)} copy(f32[144,1076]{1,0:T(8,128)} %get-tuple-element.16) | data formatting | bytes 1239552
  97.4 0.0 copy-done.1
  97.4 0.6 copy.19
  98.0 0.0 copy-done
  98.0 0.6 copy.20
Async XLA Ops:
  95.4 2.0 %copy-start.1 = (f32[144]{0:T(256)S(1)}, f32[144]{0:T(256)}, u32[]{:S(2)}) copy-start(f32[144]{0:T(256)} %get-tuple-element.17) | copy-start | bytes 1732
  95.5 2.6 %copy-start = (f32[1076]{0:T(1024)S(1)}, f32[1076]{0:T(1024)}, u32[]{:S(2)}) copy-start(f32[1076]{0:T(1024)} %get-tuple-element.18) | copy-start | bytes 12916

commit v4 on v3

--- a/solution.py
+++ b/solution.py
@@ -28,11 +28,12 @@
     upd_ref, nr_ref, nc_ref, loss_ref,
     hv, wv, pv, tv, rmv, cmv, hs, pool, rmc,
     hid, wg, txa, part, pre, summed, proj, mix, imgs, ug_s, ug_r, mg_s, mga, turned, gp, gz_s, gz,
-    rsb, csb, stb, ld,
+    rsb, csb, stb, qcb, srb, hid2, mgx_s, mgx, ld,
     hid_ss, hid_rs, hx_rs, w_ss, w_rs, tz_ss, tp_ss, t_rs, td_ss, td_rs, pp_ss, pp_rs, p_ss, p_rs, pair_ss, pair_rs,
     mg_ss, mg_rs, g_ss, g_rs, row_ss, row_rs, col_ss, col_rs, st_ss, st_rs,
+    qc_ss, qc_rs, sr_ss, sr_rs, hf_ss, hf_rs, mgx_ss, mgx_rs,
 ):
-    R, C, X, Z, T, Db, Dp, Fb, K, F2, F2p, Fw = sizes
+    R, C, X, Z, T, Db, Dp, Fb, K, E, F2, F2p, Fw = sizes
     L = LOW
     plane = R * L
     devices = R * C
@@ -156,6 +157,9 @@
     split = T // 4
     low = z < Z // 2
     final = jnp.where(low, Z - 1, 0)
+    edge = jnp.logical_and(E > 0, jnp.logical_or(z == 0, z == Z - 1))
+    nearby = jnp.logical_and(E > 0, jnp.logical_or(z == 1, z == Z - 2))
+    nest = jnp.where(low, 1, Z - 2)
 
     def relay(s):
         for d, direction in enumerate((1, -1)):
@@ -177,7 +181,7 @@
                 onward = neighbours()[X - 1:] if h == 0 else neighbours()[:X - 1]
                 for x3, y3 in onward:
                     send(
-                        half, half, td_ss, td_rs.at[jnp.where(block == final, 1, 0)],
+                        half, half, td_ss, td_rs,
                         (x3 * CORES + core, z * L + y3), has if s else None, True,
                     )
 
@@ -272,6 +276,8 @@
         relay(s - 1)
         if s == Z - 2:
             arrived(hid.at[pl.ds(0, (plane - 1 - crossing) * T)], hid_rs)
+            if E:
+                send(hid, hid2, hf_ss, hf_rs, (r, nest * L + y), edge)
             project(0)
     weights_on(Z - 1)
     project(1)
@@ -299,9 +305,9 @@
     bias = jnp.full((1, 1), bias_ref[0], F32)
     width = X * L * T
 
-    def pairs(top, count, zs):
+    def pairs(top, count, zs, blocks=1):
         images = imgs[top:top + count]
-        texts = txa[rows(zs, width)]
+        texts = txa[pl.ds(pl.multiple_of(zs * width, width), blocks * width)]
         logits = scale * dot_nt(images, texts) + bias
         row_id = lax.broadcasted_iota(jnp.int32, logits.shape, 0) + top
         col_id = lax.broadcasted_iota(jnp.int32, logits.shape, 1) + (zs * width - own_slot * T)
@@ -317,20 +323,21 @@
         loss, grads = pairs(0, 2 * T, jnp.where(low, k, Z - 1 - k))
         return carry[0] + loss, carry[1] + grads
 
-    arrived(txa.at[pl.ds(0, (Z - 1) * pairs_each)], td_rs.at[0])
+    arrived(txa.at[pl.ds(0, Z * pairs_each)], td_rs)
     arrived(theirs, pair_rs.at[0])
     carry = (jnp.zeros((2 * T, 1), F32), jnp.zeros((2 * T, L * F2), F32))
+    tail = min(Z, 2)
     if Z <= 4:
-        for k in range(Z - 1):
+        for k in range(Z - tail):
             carry = more(k, carry)
     else:
-        carry = lax.fori_loop(0, Z - 1, more, carry)
+        carry = lax.fori_loop(0, Z - tail, more, carry)
     loss_most, grads = carry
-    arrived(txa.at[pl.ds(0, pairs_each)], td_rs.at[1])
-    loss_b, grads_b = pairs(T, T, final)
+    ending = jnp.where(low, Z - tail, 0)
+    loss_b, grads_b = pairs(T, T, ending, tail)
     ug_s[...] = scale * (grads[T:] + grads_b)
     send(ug_s, ug_r, pair_ss.at[1], pair_rs.at[1], partner)
-    loss_a, grads_a = pairs(0, T, final)
+    loss_a, grads_a = pairs(0, T, ending, tail)
     arrived(ug_r, pair_rs.at[1])
     ug = scale * (grads[:T] + grads_a) + ug_r[...]
     inner = jnp.sum(unit * ug, axis=1, keepdims=True)
@@ -348,99 +355,18 @@
         )
     send(mg_s.at[y], mga.at[rows(q, T)], mg_ss, mg_rs.at[q], partner, bulk=True)
     mga[rows(q, T)] = mg_s[y]
-    for x2, y2 in others:
-        source = (x2 * CORES + core) * L + y2
-        at = mga.at[rows(source, T)]
-        arrived(at, mg_rs.at[source])
-        send(at, at, mg_ss, mg_rs.at[source], partner, bulk=True)
-    sent(mga.at[pl.ds(0, (plane - 1) * T)], mg_ss)
-    for x2, y2 in [(x, y)] + others:
-        source = (x2 * CORES + 1 - core) * L + y2
-        arrived(mga.at[rows(source, T)], mg_rs.at[source])
-
-    turned[...] = mga[...].T
-
-    def own_part(zd):
-        gp[zd] = jnp.dot(turned[rows(zd, Dp)], hid[...], preferred_element_type=F32)
-
-    def pieces(tau, d):
-        place = z if d == 0 else Z - 1 - z
-        i = tau - 2 * place
-        zd = jnp.clip(i, 0, Z * K - 1) // K
-        k = jnp.clip(i, 0, Z * K - 1) % K
-        zd = Z - 1 - zd if d == 0 else zd
-        beyond = zd > z if d == 0 else zd < z
-        ready = jnp.logical_and(i >= 0, i < Z * K)
-        cut = rows(k, Dc)
-        copy = pltpu.make_async_remote_copy(
-            src_ref=gz_s.at[zd, cut], dst_ref=gz.at[d, zd, cut],
-            send_sem=g_ss, recv_sem=g_rs.at[d, zd, k],
-            device_id=(r, jnp.clip(z + (1 if d == 0 else -1), 0, Z - 1) * L + y), device_id_type=MESH,
-        )
-        return place, zd, k, cut, jnp.logical_and(ready, beyond), jnp.logical_and(ready, zd == z), copy
-
-    def step(tau, _):
-        for d in range(2):
-            place, zd, k, cut, passing, ending, copy = pieces(tau, d)
-            at = gz.at[d, zd, cut]
-
-            def first():
-                gz_s[zd, cut] = gp[zd, cut].astype(BF16)
-                copy.start()
-
-            def onward():
-                arrived(at, g_rs.at[d, zd, k])
-                gz_s[zd, cut] = (gp[zd, cut] + at[...].astype(F32)).astype(BF16)
-                copy.start()
-
-            def last():
-                arrived(at, g_rs.at[d, zd, k])
-                gp[zd, cut] = gp[zd, cut] + at[...].astype(F32)
-
-            pl.when(jnp.logical_and(passing, place == 0))(first)
-            pl.when(jnp.logical_and(passing, place > 0))(onward)
-            pl.when(jnp.logical_and(ending, place > 0))(last)
-        return _
-
-    steps_g = max((Z - 1) * K + 1, K - 1 + 2 * (Z - 1)) + 1
-    head = min(K, 2)
-
-    def order(k):
-        return jnp.where(z < (Z + 1) // 2, Z - 1 - k, k)
-
-    own_part(order(0))
-    lax.fori_loop(0, head, step, 0)
-    for k in range(1, Z):
-        own_part(order(k))
-    sent(gz_s.at[pl.ds(0, Z - 1)], g_ss)
-    lax.fori_loop(head, steps_g, step, 0)
-    g = gp[z][:Db]
-
-    sq = g * g + FLOOR_VALUE
-    rsb[r] = jnp.sum(sq, axis=1, keepdims=True)
-    csb[c] = jnp.sum(sq, axis=0, keepdims=True)
-    for o in range(1, C):
-        c2 = lax.rem(c + o, C)
-        send(csb.at[c], csb.at[c], col_ss, col_rs, (r, c2), bulk=True)
-    for o in range(1, R):
-        r2 = lax.rem(r + o, R)
-        send(rsb.at[r], rsb.at[r], row_ss, row_rs, (r2, c), bulk=True)
-    sent(csb.at[pl.ds(0, C - 1)], col_ss)
-    sent(rsb.at[pl.ds(0, R - 1)], row_ss)
-    arrived(rsb.at[pl.ds(0, R - 1)], row_rs)
-    arrived(csb.at[pl.ds(0, C - 1)], col_rs)
-    row_sum = sum(rsb[k] for k in range(R))
-    col_sum = sum(csb[k] for k in range(C))
-    new_row = DECAY_RATE * rmc[...] + (1.0 - DECAY_RATE) * row_sum / (R * Fb)
-    new_col = DECAY_RATE * cmv[...].reshape(1, Fb) + (1.0 - DECAY_RATE) * col_sum / (C * Db)
-    nr_ref[...] = jnp.sum(jnp.where(eye, new_row, 0.0), axis=0)
-    nc_ref[...] = new_col[0]
-    raw = g / jnp.sqrt(new_row * new_col)
-    upd_ref[...] = raw
-    local = jnp.sum(jnp.sum(raw * raw, axis=1, keepdims=True), axis=0, keepdims=True)
+    everyone = others + [(x, y)]
+    if E:
+        for h in range(L):
+            top = mg[:, h * F2 + (Z - 1) * Dp:h * F2 + Z * Dp]
+            mgx_s[h] = jnp.where(low, top, mg[:, h * F2:h * F2 + Dp])
+        for x2, y2 in everyone:
+            send(
+                mgx_s.at[y2], mgx.at[rows(q, T)], mgx_ss, mgx_rs.at[q],
+                (x2 * CORES + core, nest * L + y2), edge, True,
+            )
     loss_local = jnp.sum(loss_a + loss_b, axis=0, keepdims=True) + jnp.sum(loss_most, axis=0, keepdims=True)
-    lane = lax.broadcasted_iota(jnp.int32, (1, 128), 1)
-    stb[me] = jnp.where(lane == 0, local, loss_local)
+    stb[me] = jnp.broadcast_to(loss_local, (1, 128))
 
     def tell(o, _):
         other = lax.rem(me + o, devices)
@@ -450,12 +376,148 @@
         ).start()
         return _
 
-    lax.fori_loop(1, devices, tell, 0)
+    for x2, y2 in others:
+        source = (x2 * CORES + core) * L + y2
+        at = mga.at[rows(source, T)]
+        arrived(at, mg_rs.at[source])
+        send(at, at, mg_ss, mg_rs.at[source], partner, bulk=True)
+    sent(mga.at[pl.ds(0, (plane - 1) * T)], mg_ss)
+    if E:
+        finish.append(lambda: pl.when(jnp.logical_or(edge, nearby))(
+            lambda: arrived(mgx.at[pl.ds(0, X * L * T)], mgx_ss)
+        ))
+    for x2, y2 in [(x, y)] + others:
+        source = (x2 * CORES + 1 - core) * L + y2
+        arrived(mga.at[rows(source, T)], mg_rs.at[source])
+
+    turned[...] = mga[...].T
+
+    def own_part(zd):
+        gp[zd] = jnp.dot(turned[rows(zd, Dp)], hid[...], preferred_element_type=F32)
+
+    def far_part():
+        for x2, y2 in everyone:
+            at = mgx.at[rows((x2 * CORES + core) * L + y2, T)]
+            arrived(at, mgx_rs.at[(x2 * CORES + core) * L + y2])
+            send(at, at, mgx_ss, mgx_rs.at[(x2 * CORES + core) * L + y2], partner, bulk=True)
+        arrived(hid2, hf_rs)
+        for x2, y2 in everyone:
+            source = (x2 * CORES + 1 - core) * L + y2
+            arrived(mgx.at[rows(source, T)], mgx_rs.at[source])
+        gp[final] = gp[final] + jnp.dot(mgx[...].T, hid2[...], preferred_element_type=F32)
+
+    def pieces(tau, d):
+        place = z if d == 0 else Z - 1 - z
+        far = Z - 1 if d == 0 else 0
+        i = tau - 2 * jnp.maximum(place - E, 0) + jnp.where(place == 0, K * E, 0)
+        zd = jnp.clip(i, 0, Z * K - 1) // K
+        k = jnp.clip(i, 0, Z * K - 1) % K
+        zd = Z - 1 - zd if d == 0 else zd
+        beyond = zd > z if d == 0 else zd < z
+        ready = jnp.logical_and(i >= 0, i < Z * K)
+        opens = jnp.logical_or(place == 0, jnp.logical_and(place == E, zd == far))
+        return zd, k, jnp.logical_and(ready, beyond), jnp.logical_and(ready, zd == z), opens, place
+
+    def step(tau, held):
+        for d in range(2):
+            zd, k, passing, ending, opens, place = pieces(tau, d)
+            cut = rows(k, Dc)
+            at = gz.at[d, zd, cut]
+            copy = pltpu.make_async_remote_copy(
+                src_ref=gz_s.at[zd, cut], dst_ref=at, send_sem=g_ss, recv_sem=g_rs.at[d, zd, k],
+                device_id=(r, jnp.clip(z + (1 if d == 0 else -1), 0, Z - 1) * L + y), device_id_type=MESH,
+            )
+
+            def first():
+                gz_s[zd, cut] = gp[zd, cut].astype(BF16)
+                copy.start()
+
+            def onward():
+                arrived(at, g_rs.at[d, zd, k])
+                gz_s[zd, cut] = (gp[zd, cut] + at[...].astype(F32)).astype(BF16)
+                copy.start()
+
+            def last():
+                arrived(at, g_rs.at[d, zd, k])
+                gp[zd, cut] = gp[zd, cut] + at[...].astype(F32)
+
+            passing = jnp.logical_and(passing, held)
+            ending = jnp.logical_and(jnp.logical_and(ending, held), place > 0)
+            pl.when(jnp.logical_and(passing, opens))(first)
+            pl.when(jnp.logical_and(passing, jnp.logical_not(opens)))(onward)
+            pl.when(ending)(last)
+
+    def early(tau, _):
+        step(tau, edge)
+        return _
+
+    def later(tau, _):
+        step(tau, jnp.logical_or(jnp.logical_not(edge), tau >= head))
+        return _
+
+    steps_g = max((Z - 1) * K + 1 - 2 * E, K - 1 + 2 * (Z - 1 - E)) + 1
+    head = min(K, 2)
+
+    def order(k):
+        return jnp.where(low, Z - 1 - k, k)
+
+    if E:
+        own_part(order(1))
+        lax.fori_loop(0, head, early, 0)
+        pl.when(jnp.logical_not(edge))(lambda: own_part(order(0)))
+        for k in range(2, Z):
+            own_part(order(k))
+        lax.fori_loop(1, devices, tell, 0)
+        pl.when(nearby)(far_part)
+        finish.append(lambda: pl.when(edge)(lambda: arrived(gz_s.at[pl.ds(0, Z - 2)], g_ss)))
+        finish.append(lambda: pl.when(jnp.logical_not(edge))(lambda: arrived(gz_s.at[pl.ds(0, Z - 1)], g_ss)))
+    else:
+        for k in range(Z):
+            own_part(order(k))
+        lax.fori_loop(1, devices, tell, 0)
+        sent(gz_s.at[pl.ds(0, Z - 1)], g_ss)
+    lax.fori_loop(0, steps_g, later, 0)
+    g = gp[z][:Db]
+
+    def across_cols(box, ss, rs):
+        for o in range(1, C):
+            send(box.at[c], box.at[c], ss, rs, (r, lax.rem(c + o, C)), bulk=True)
+        sent(box.at[pl.ds(0, C - 1)], ss)
+
+    def across_rows(box, ss, rs, also=lambda: None):
+        for o in range(1, R):
+            send(box.at[r], box.at[r], ss, rs, (lax.rem(r + o, R), c), bulk=True)
+        sent(box.at[pl.ds(0, R - 1)], ss)
+        also()
+        arrived(box.at[pl.ds(0, R - 1)], rs)
+
+    square = g * g
+    sq = square + FLOOR_VALUE
+    rsb[r] = jnp.sum(jnp.where(eye, jnp.sum(sq, axis=1, keepdims=True), 0.0), axis=0, keepdims=True)
+    csb[c] = jnp.sum(sq, axis=0, keepdims=True)
+    across_rows(rsb, row_ss, row_rs, lambda: across_cols(csb, col_ss, col_rs))
+    row_sum = jnp.broadcast_to(sum(rsb[k] for k in range(R)), (Db, Db))
+    row_sum = jnp.sum(jnp.where(eye, row_sum, 0.0), axis=1, keepdims=True)
+    new_row = DECAY_RATE * rmc[...] + (1.0 - DECAY_RATE) * row_sum / (R * Fb)
+    qcb[c] = jnp.sum(square / new_row, axis=0, keepdims=True)
+    across_cols(qcb, qc_ss, qc_rs)
+    nr_ref[...] = jnp.sum(jnp.where(eye, new_row, 0.0), axis=0)
+    arrived(csb.at[pl.ds(0, C - 1)], col_rs)
+    col_sum = sum(csb[k] for k in range(C))
+    new_col = DECAY_RATE * cmv[...].reshape(1, Fb) + (1.0 - DECAY_RATE) * col_sum / (C * Db)
+    nc_ref[...] = new_col[0]
+    upd_ref[...] = g / jnp.sqrt(new_row * new_col)
+    arrived(qcb.at[pl.ds(0, C - 1)], qc_rs)
+    part_sum = jnp.sum(sum(qcb[k] for k in range(C)) / new_col, axis=1, keepdims=True)
+    srb[r] = jnp.broadcast_to(part_sum, (1, 128))
+    across_rows(srb, sr_ss, sr_rs)
+    total = sum(srb[k] for k in range(R))[:, 0:1]
+    rms = jnp.sqrt(total / (C * Db * R * Fb))
+    upd_ref[...] = upd_ref[...] / jnp.maximum(1.0, rms / CLIP_LEVEL)
     sent(stb.at[pl.ds(0, devices - 1)], st_ss)
     arrived(stb.at[pl.ds(0, devices - 1)], st_rs)
+    lane = lax.broadcasted_iota(jnp.int32, (1, 128), 1)
     totals = jnp.sum(stb[...], axis=0)
-    rms = jnp.sqrt(totals[:, 0:1] / (C * Db * R * Fb))
-    upd_ref[...] = upd_ref[...] / jnp.maximum(1.0, rms / CLIP_LEVEL)
     loss_ref[0] = jnp.sum(jnp.where(lane == 1, totals, 0.0)) / batch
     for wait in finish:
         wait()
@@ -472,9 +534,10 @@
     texts = X * C * T
 
     K = 3 if Dp % 48 == 0 else 1
+    E = 1 if Z >= 4 else 0
     F2p = -(-F2 // 128) * 128
     Fw = max(-(-Dp // 128) * 128, F2p - (F2 - Dp) // 128 * 128)
-    sizes = (R, C, X, Z, T, Db, Dp, Fb, K, F2, F2p, Fw)
+    sizes = (R, C, X, Z, T, Db, Dp, Fb, K, E, F2, F2p, Fw)
     vmem = pl.BlockSpec(memory_space=pltpu.VMEM)
     smem = pl.BlockSpec(memory_space=pltpu.SMEM)
     dma = lambda *s: pltpu.SemaphoreType.DMA(s)
@@ -516,13 +579,19 @@
             pltpu.VMEM((Z, Dp, Fb), F32),
             pltpu.VMEM((Z, Dp, Fb), BF16),
             pltpu.VMEM((2, Z, Dp, Fb), BF16),
-            pltpu.VMEM((R, Db, 1), F32),
+            pltpu.VMEM((R, 1, Db), F32),
             pltpu.VMEM((C, 1, Fb), F32),
             pltpu.VMEM((R * C, 1, 128), F32),
+            pltpu.VMEM((C, 1, Fb), F32),
+            pltpu.VMEM((R, 1, 128), F32),
+            pltpu.VMEM((plane * T, Fb), BF16),
+            pltpu.VMEM((L, T, Dp), BF16),
+            pltpu.VMEM((plane * T, Dp), BF16),
             dma(6),
-            one, one, one, dma(2, Z), dma(Z), dma(2, Z), one, dma(X * C), one, dma(2),
+            one, one, one, dma(2, Z), dma(Z), dma(2, Z), one, dma(X * C), one, one,
             one, dma(X, 2), one, dma(2), dma(2), dma(2),
             one, dma(plane), one, dma(2, Z, K), one, one, one, one, one, one,
+            one, one, one, one, one, one, one, dma(plane),
         ],
         compiler_params=pltpu.CompilerParams(
             has_side_effects=True, collective_id=0, vmem_limit_bytes=60 * 1024 * 1024

time: 101 us -> 93.6 us (0.927)
  Pallas kernels: 93.5 us -> 86.5 us
    pallas_call x1, Pallas kernels: 93.5 us -> 86.5 us  [per_device(): pl.pallas_call(functools.partial(kernel, sizes), out_shape=(jax.ShapeDtyp...]
where the time goes in v4:
time: 93.6 us; the launch traced here: 93.4 us
  Pallas kernels  86.5 us (92%)
  between operations  3.75 us (4%)
  local copies, waits for them, and re-layouts  3.15 us (3%)
    pallas_call x1, Pallas kernels, per_device(): pl.pallas_call(functools.partial(kernel, sizes), out_shape=(jax.ShapeDtyp...  86.5 us
    unnamed x7, local copies, waits for them, and re-layouts  3.15 us

profile of v4, /device:TPU:0, one launch (start us, length us, event | category | flops | bytes accessed | tf_op | source)
XLA Modules:
  0.0 93.4 jit_solution(5771066043617757754)
XLA Ops:
  1.9 86.5 %shard_map.111 = (f32[144,1076]{1,0:T(8,128)}, f32[144]{0:T(256)}, f32[1076]{0:T(1024)}, f32[1]{0:T(128)}) custom-call(bf16[64,4304]{1,0:T(8,128)(2,1)} %hid_in.1, f32[144,1076]{1,0:T(8,128)} %w_in.1, bf16[64,1152]{1,0:T(8,128)(2,1)} %pool_in.1, bf16[64,1152]{1,0:T(8,128)(2,1)} %text_in.1, f32[144]{0:T(256)} %rm_in.1, f32[1076]{0:T(1024)} %cm_in.1, ...), custom_call_target="tpu_custom_call" | custom-call | tf_op jit(solution)/shard_map/pallas_call | solution.py:545
  88.4 0.0 copy-start.1
  88.4 0.0 copy-start
  88.4 2.0 %copy.18 = f32[144,1076]{1,0:T(8,128)} copy(f32[144,1076]{1,0:T(8,128)} %get-tuple-element.16) | data formatting | bytes 1239552
  90.4 0.0 copy-done.1
  90.4 0.6 copy.19
  91.0 0.0 copy-done
  91.0 0.6 copy.20
Async XLA Ops:
  88.4 2.0 %copy-start.1 = (f32[144]{0:T(256)S(1)}, f32[144]{0:T(256)}, u32[]{:S(2)}) copy-start(f32[144]{0:T(256)} %get-tuple-element.17) | copy-start | bytes 1732
  88.4 2.6 %copy-start = (f32[1076]{0:T(1024)S(1)}, f32[1076]{0:T(1024)}, u32[]{:S(2)}) copy-start(f32[1076]{0:T(1024)} %get-tuple-element.18) | copy-start | bytes 12916

commit v5 on v4

--- a/solution.py
+++ b/solution.py
@@ -25,10 +25,10 @@
 def kernel(
     sizes,
     hid_in, w_in, pool_in, text_in, rm_in, cm_in, ls_ref, bias_ref,
-    upd_ref, nr_ref, nc_ref, loss_ref,
+    upd_out, nr_out, nc_out, end_ref,
     hv, wv, pv, tv, rmv, cmv, hs, pool, rmc,
     hid, wg, txa, part, pre, summed, proj, mix, imgs, ug_s, ug_r, mg_s, mga, turned, gp, gz_s, gz,
-    rsb, csb, stb, qcb, srb, hid2, mgx_s, mgx, ld,
+    upd_ref, nr_ref, nc_ref, rsb, csb, stb, qcb, srb, hid2, mgx_s, mgx, ld,
     hid_ss, hid_rs, hx_rs, w_ss, w_rs, tz_ss, tp_ss, t_rs, td_ss, td_rs, pp_ss, pp_rs, p_ss, p_rs, pair_ss, pair_rs,
     mg_ss, mg_rs, g_ss, g_rs, row_ss, row_rs, col_ss, col_rs, st_ss, st_rs,
     qc_ss, qc_rs, sr_ss, sr_rs, hf_ss, hf_rs, mgx_ss, mgx_rs,
@@ -507,20 +507,31 @@
     new_col = DECAY_RATE * cmv[...].reshape(1, Fb) + (1.0 - DECAY_RATE) * col_sum / (C * Db)
     nc_ref[...] = new_col[0]
     upd_ref[...] = g / jnp.sqrt(new_row * new_col)
+    for i, (src, dst) in enumerate(((upd_ref, upd_out), (nr_ref, nr_out), (nc_ref, nc_out))):
+        store = pltpu.make_async_copy(src, dst, ld.at[6 + i])
+        store.start()
+        finish.append(store.wait)
     arrived(qcb.at[pl.ds(0, C - 1)], qc_rs)
     part_sum = jnp.sum(sum(qcb[k] for k in range(C)) / new_col, axis=1, keepdims=True)
     srb[r] = jnp.broadcast_to(part_sum, (1, 128))
     across_rows(srb, sr_ss, sr_rs)
     total = sum(srb[k] for k in range(R))[:, 0:1]
     rms = jnp.sqrt(total / (C * Db * R * Fb))
-    upd_ref[...] = upd_ref[...] / jnp.maximum(1.0, rms / CLIP_LEVEL)
+    end_ref[0] = jnp.max(jnp.maximum(1.0, rms / CLIP_LEVEL))
     sent(stb.at[pl.ds(0, devices - 1)], st_ss)
     arrived(stb.at[pl.ds(0, devices - 1)], st_rs)
     lane = lax.broadcasted_iota(jnp.int32, (1, 128), 1)
     totals = jnp.sum(stb[...], axis=0)
-    loss_ref[0] = jnp.sum(jnp.where(lane == 1, totals, 0.0)) / batch
+    end_ref[1] = jnp.sum(jnp.where(lane == 1, totals, 0.0)) / batch
     for wait in finish:
         wait()
+
+
+def divide(raw_ref, row_ref, col_ref, end_ref, upd_ref, nr_ref, nc_ref, loss_ref):
+    upd_ref[...] = raw_ref[...] / end_ref[0]
+    nr_ref[...] = row_ref[...]
+    nc_ref[...] = col_ref[...]
+    loss_ref[0] = end_ref[1]
 
 
 def per_device(pooled, hidden, text, weight, row_moment, col_moment, log_scale, bias):
@@ -542,16 +553,16 @@
     smem = pl.BlockSpec(memory_space=pltpu.SMEM)
     dma = lambda *s: pltpu.SemaphoreType.DMA(s)
     one = pltpu.SemaphoreType.DMA
-    upd, nr, nc, loss = pl.pallas_call(
+    raw = pl.pallas_call(
         functools.partial(kernel, sizes),
         out_shape=(
             jax.ShapeDtypeStruct((Db, Fb), F32),
             jax.ShapeDtypeStruct((Db,), F32),
             jax.ShapeDtypeStruct((Fb,), F32),
-            jax.ShapeDtypeStruct((1,), F32),
+            jax.ShapeDtypeStruct((2,), F32),
         ),
         in_specs=[pl.BlockSpec(memory_space=pl.ANY)] * 6 + [smem] * 2,
-        out_specs=(vmem,) * 3 + (smem,),
+        out_specs=(pl.BlockSpec(memory_space=pl.ANY),) * 3 + (smem,),
         scratch_shapes=[
             pltpu.VMEM((T, R * Fb), BF16),
             pltpu.VMEM((Db, Fb), F32),
@@ -579,6 +590,9 @@
             pltpu.VMEM((Z, Dp, Fb), F32),
             pltpu.VMEM((Z, Dp, Fb), BF16),
             pltpu.VMEM((2, Z, Dp, Fb), BF16),
+            pltpu.VMEM((Db, Fb), F32),
+            pltpu.VMEM((Db,), F32),
+            pltpu.VMEM((Fb,), F32),
             pltpu.VMEM((R, 1, Db), F32),
             pltpu.VMEM((C, 1, Fb), F32),
             pltpu.VMEM((R * C, 1, 128), F32),
@@ -587,7 +601,7 @@
             pltpu.VMEM((plane * T, Fb), BF16),
             pltpu.VMEM((L, T, Dp), BF16),
             pltpu.VMEM((plane * T, Dp), BF16),
-            dma(6),
+            dma(9),
             one, one, one, dma(2, Z), dma(Z), dma(2, Z), one, dma(X * C), one, one,
             one, dma(X, 2), one, dma(2), dma(2), dma(2),
             one, dma(plane), one, dma(2, Z, K), one, one, one, one, one, one,
@@ -599,6 +613,17 @@
     )(
         hidden, weight, pooled, text, row_moment, col_moment, log_scale[None], bias[None],
     )
+    upd, nr, nc, loss = pl.pallas_call(
+        divide,
+        out_shape=(
+            jax.ShapeDtypeStruct((Db, Fb), F32),
+            jax.ShapeDtypeStruct((Db,), F32),
+            jax.ShapeDtypeStruct((Fb,), F32),
+            jax.ShapeDtypeStruct((1,), F32),
+        ),
+        in_specs=[vmem] * 3 + [smem],
+        out_specs=(vmem,) * 3 + (smem,),
+    )(*raw)
     return upd, nr, nc, loss[0]
 
 

time: 93.6 us -> 90.2 us (0.964)
  local copies, waits for them, and re-layouts: 3.15 us -> 0 us
  between operations: 3.75 us -> 1.93 us
  Pallas kernels: 86.5 us -> 88.1 us
    unnamed x7 -> x0, local copies, waits for them, and re-layouts: 3.15 us -> none
    pallas_call x0 -> x1, Pallas kernels: none -> 2.01 us  [per_device(): pl.pallas_call(divide, out_shape=(jax.ShapeDtypeStruct((Db, Fb), F32), ja...]
where the time goes in v5:
time: 90.2 us; the launch traced here: 90 us
  Pallas kernels  88.1 us (98%)
  between operations  1.93 us (2%)
    pallas_call x1, Pallas kernels, per_device(): pl.pallas_call(functools.partial(kernel, sizes), out_shape=(jax.ShapeDtyp...  86.1 us
    pallas_call x1, Pallas kernels, per_device(): pl.pallas_call(divide, out_shape=(jax.ShapeDtypeStruct((Db, Fb), F32), ja...  2.01 us

profile of v5, /device:TPU:0, one launch (start us, length us, event | category | flops | bytes accessed | tf_op | source)
XLA Modules:
  0.0 90.0 jit_solution(3574312677644088084)
XLA Ops:
  1.9 86.1 %shard_map.111 = (f32[144,1076]{1,0:T(8,128)}, f32[144]{0:T(256)}, f32[1076]{0:T(1024)}, f32[2]{0:T(128)}) custom-call(bf16[64,4304]{1,0:T(8,128)(2,1)} %hid_in.1, f32[144,1076]{1,0:T(8,128)} %w_in.1, bf16[64,1152]{1,0:T(8,128)(2,1)} %pool_in.1, bf16[64,1152]{1,0:T(8,128)(2,1)} %text_in.1, f32[144]{0:T(256)} %rm_in.1, f32[1076]{0:T(1024)} %cm_in.1, ...), custom_call_target="tpu_custom_call" | custom-call | tf_op jit(solution)/shard_map/pallas_call | solution.py:556
  88.0 2.0 %shard_map.112 = (f32[144,1076]{1,0:T(8,128)}, f32[144]{0:T(256)}, f32[1076]{0:T(1024)}, f32[1]{0:T(128)}) custom-call(f32[144,1076]{1,0:T(8,128)} %get-tuple-element.12.raw_ref, f32[144]{0:T(256)} %get-tuple-element.13.row_ref, f32[1076]{0:T(1024)} %get-tuple-element.14.col_ref, f32[2]{0:T(128)} %get-tuple-element.15.end_ref), custom_call_target="tpu_custom_call" | custom-call | tf_op jit(solution)/shard_map/pallas_call | solution.py:616

commit v6 on v5

--- a/solution.py
+++ b/solution.py
@@ -28,9 +28,9 @@
     upd_out, nr_out, nc_out, end_ref,
     hv, wv, pv, tv, rmv, cmv, hs, pool, rmc,
     hid, wg, txa, part, pre, summed, proj, mix, imgs, ug_s, ug_r, mg_s, mga, turned, gp, gz_s, gz,
-    upd_ref, nr_ref, nc_ref, rsb, csb, stb, qcb, srb, hid2, mgx_s, mgx, ld,
+    upd_ref, nr_ref, nc_ref, end_v, rsb, csb, qcb, srb, hid2, mgx_s, mgx, ld,
     hid_ss, hid_rs, hx_rs, w_ss, w_rs, tz_ss, tp_ss, t_rs, td_ss, td_rs, pp_ss, pp_rs, p_ss, p_rs, pair_ss, pair_rs,
-    mg_ss, mg_rs, g_ss, g_rs, row_ss, row_rs, col_ss, col_rs, st_ss, st_rs,
+    mg_ss, mg_rs, g_ss, g_rs, row_ss, row_rs, col_ss, col_rs,
     qc_ss, qc_rs, sr_ss, sr_rs, hf_ss, hf_rs, mgx_ss, mgx_rs,
 ):
     R, C, X, Z, T, Db, Dp, Fb, K, E, F2, F2p, Fw = sizes
@@ -44,7 +44,6 @@
     x, core = r // CORES, r % CORES
     q = r * L + y
     finish = []
-    me = r * C + c
     Dc = Dp // K
 
     loads = [
@@ -154,7 +153,6 @@
         along_x = [(lax.rem(x + o, X), y) for o in range(1, X)]
         return along_x + [(x, lax.rem(y + o, L)) for o in range(1, L)]
 
-    split = T // 4
     low = z < Z // 2
     final = jnp.where(low, Z - 1, 0)
     edge = jnp.logical_and(E > 0, jnp.logical_or(z == 0, z == Z - 1))
@@ -162,6 +160,7 @@
     nest = jnp.where(low, 1, Z - 2)
 
     def relay(s):
+        split = T // 4 if s < 2 else T // 2
         for d, direction in enumerate((1, -1)):
             if s == 0 and d:
                 continue
@@ -236,13 +235,13 @@
     def project(g):
         start, width = spans[g]
         lanes = pl.ds(start, width)
-        part[:, lanes] = dot_nt(hid[...], wg[lanes])
-        for o in range(1, X + 1):
-            x2 = lax.rem(x + o, X)
-            send(
-                part.at[rows(x2 * CORES + 1 - core, L * T), lanes], pre.at[x2, :, lanes],
-                pp_ss, pp_rs.at[x2, g], partner, bulk=True,
-            )
+        for side in (1 - core, core):
+            for o in range(1, X + 1):
+                x2 = lax.rem(x + o, X)
+                at = rows(x2 * CORES + side, L * T)
+                part[at, lanes] = dot_nt(hid[at], wg[lanes])
+                if side is not core:
+                    send(part.at[at, lanes], pre.at[x2, :, lanes], pp_ss, pp_rs.at[x2, g], partner, bulk=True)
 
     def spread(g):
         start, width = spans[g]
@@ -319,27 +318,26 @@
         pg = (jnp.where(match, -sig, sig) / batch).astype(BF16)
         return loss, jnp.dot(pg, texts, preferred_element_type=F32)
 
-    def more(k, carry):
-        loss, grads = pairs(0, 2 * T, jnp.where(low, k, Z - 1 - k))
-        return carry[0] + loss, carry[1] + grads
-
+    def total(top):
+        loss, grads = pairs(top, T, 0, wide)
+        if Z <= wide:
+            return loss, grads
+
+        def more(k, carry):
+            loss, grads = pairs(top, T, k * wide, wide)
+            return carry[0] + loss, carry[1] + grads
+
+        return lax.fori_loop(1, Z // wide, more, (loss, grads))
+
+    wide = max(w for w in (1, 2, 4) if Z % w == 0)
     arrived(txa.at[pl.ds(0, Z * pairs_each)], td_rs)
+    loss_a, grads_a = total(0)
     arrived(theirs, pair_rs.at[0])
-    carry = (jnp.zeros((2 * T, 1), F32), jnp.zeros((2 * T, L * F2), F32))
-    tail = min(Z, 2)
-    if Z <= 4:
-        for k in range(Z - tail):
-            carry = more(k, carry)
-    else:
-        carry = lax.fori_loop(0, Z - tail, more, carry)
-    loss_most, grads = carry
-    ending = jnp.where(low, Z - tail, 0)
-    loss_b, grads_b = pairs(T, T, ending, tail)
-    ug_s[...] = scale * (grads[T:] + grads_b)
+    loss_b, grads_b = total(T)
+    ug_s[...] = scale * grads_b
     send(ug_s, ug_r, pair_ss.at[1], pair_rs.at[1], partner)
-    loss_a, grads_a = pairs(0, T, ending, tail)
     arrived(ug_r, pair_rs.at[1])
-    ug = scale * (grads[:T] + grads_a) + ug_r[...]
+    ug = scale * grads_a + ug_r[...]
     inner = jnp.sum(unit * ug, axis=1, keepdims=True)
     mg = ((ug - unit * inner) / length).astype(BF16)
     for h in range(L):
@@ -348,13 +346,6 @@
         (lax.rem(x + ox, X), lax.rem(y + oy, L))
         for ox in reversed(range(X)) for oy in reversed(range(L)) if ox or oy
     ]
-    for x2, y2 in others:
-        send(
-            mg_s.at[y2], mga.at[rows(q, T)], mg_ss, mg_rs.at[q],
-            (x2 * CORES + core, z * L + y2), bulk=True,
-        )
-    send(mg_s.at[y], mga.at[rows(q, T)], mg_ss, mg_rs.at[q], partner, bulk=True)
-    mga[rows(q, T)] = mg_s[y]
     everyone = others + [(x, y)]
     if E:
         for h in range(L):
@@ -365,17 +356,15 @@
                 mgx_s.at[y2], mgx.at[rows(q, T)], mgx_ss, mgx_rs.at[q],
                 (x2 * CORES + core, nest * L + y2), edge, True,
             )
-    loss_local = jnp.sum(loss_a + loss_b, axis=0, keepdims=True) + jnp.sum(loss_most, axis=0, keepdims=True)
-    stb[me] = jnp.broadcast_to(loss_local, (1, 128))
-
-    def tell(o, _):
-        other = lax.rem(me + o, devices)
-        pltpu.make_async_remote_copy(
-            src_ref=stb.at[me], dst_ref=stb.at[me], send_sem=st_ss, recv_sem=st_rs,
-            device_id=(other // C, other % C), device_id_type=MESH,
-        ).start()
-        return _
-
+    for x2, y2 in others:
+        send(
+            mg_s.at[y2], mga.at[rows(q, T)], mg_ss, mg_rs.at[q],
+            (x2 * CORES + core, z * L + y2), bulk=True,
+        )
+    send(mg_s.at[y], mga.at[rows(q, T)], mg_ss, mg_rs.at[q], partner, bulk=True)
+    mga[rows(q, T)] = mg_s[y]
+    loss_local = jnp.sum(loss_a + loss_b, axis=0, keepdims=True)
+    csb[c, :, Fb:Fb + 1] = loss_local
     for x2, y2 in others:
         source = (x2 * CORES + core) * L + y2
         at = mga.at[rows(source, T)]
@@ -424,7 +413,7 @@
             cut = rows(k, Dc)
             at = gz.at[d, zd, cut]
             copy = pltpu.make_async_remote_copy(
-                src_ref=gz_s.at[zd, cut], dst_ref=at, send_sem=g_ss, recv_sem=g_rs.at[d, zd, k],
+                src_ref=gz_s.at[zd, cut], dst_ref=at, send_sem=g_ss, recv_sem=g_rs.at[zd + 1 - d, k],
                 device_id=(r, jnp.clip(z + (1 if d == 0 else -1), 0, Z - 1) * L + y), device_id_type=MESH,
             )
 
@@ -433,12 +422,12 @@
                 copy.start()
 
             def onward():
-                arrived(at, g_rs.at[d, zd, k])
+                arrived(at, g_rs.at[zd + 1 - d, k])
                 gz_s[zd, cut] = (gp[zd, cut] + at[...].astype(F32)).astype(BF16)
                 copy.start()
 
             def last():
-                arrived(at, g_rs.at[d, zd, k])
+                arrived(at, g_rs.at[zd + 1 - d, k])
                 gp[zd, cut] = gp[zd, cut] + at[...].astype(F32)
 
             passing = jnp.logical_and(passing, held)
@@ -467,14 +456,12 @@
         pl.when(jnp.logical_not(edge))(lambda: own_part(order(0)))
         for k in range(2, Z):
             own_part(order(k))
-        lax.fori_loop(1, devices, tell, 0)
         pl.when(nearby)(far_part)
         finish.append(lambda: pl.when(edge)(lambda: arrived(gz_s.at[pl.ds(0, Z - 2)], g_ss)))
         finish.append(lambda: pl.when(jnp.logical_not(edge))(lambda: arrived(gz_s.at[pl.ds(0, Z - 1)], g_ss)))
     else:
         for k in range(Z):
             own_part(order(k))
-        lax.fori_loop(1, devices, tell, 0)
         sent(gz_s.at[pl.ds(0, Z - 1)], g_ss)
     lax.fori_loop(0, steps_g, later, 0)
     g = gp[z][:Db]
@@ -494,7 +481,7 @@
     square = g * g
     sq = square + FLOOR_VALUE
     rsb[r] = jnp.sum(jnp.where(eye, jnp.sum(sq, axis=1, keepdims=True), 0.0), axis=0, keepdims=True)
-    csb[c] = jnp.sum(sq, axis=0, keepdims=True)
+    csb[c, :, :Fb] = jnp.sum(sq, axis=0, keepdims=True)
     across_rows(rsb, row_ss, row_rs, lambda: across_cols(csb, col_ss, col_rs))
     row_sum = jnp.broadcast_to(sum(rsb[k] for k in range(R)), (Db, Db))
     row_sum = jnp.sum(jnp.where(eye, row_sum, 0.0), axis=1, keepdims=True)
@@ -504,7 +491,7 @@
     nr_ref[...] = jnp.sum(jnp.where(eye, new_row, 0.0), axis=0)
     arrived(csb.at[pl.ds(0, C - 1)], col_rs)
     col_sum = sum(csb[k] for k in range(C))
-    new_col = DECAY_RATE * cmv[...].reshape(1, Fb) + (1.0 - DECAY_RATE) * col_sum / (C * Db)
+    new_col = DECAY_RATE * cmv[...].reshape(1, Fb) + (1.0 - DECAY_RATE) * col_sum[:, :Fb] / (C * Db)
     nc_ref[...] = new_col[0]
     upd_ref[...] = g / jnp.sqrt(new_row * new_col)
     for i, (src, dst) in enumerate(((upd_ref, upd_out), (nr_ref, nr_out), (nc_ref, nc_out))):
@@ -513,25 +500,25 @@
         finish.append(store.wait)
     arrived(qcb.at[pl.ds(0, C - 1)], qc_rs)
     part_sum = jnp.sum(sum(qcb[k] for k in range(C)) / new_col, axis=1, keepdims=True)
-    srb[r] = jnp.broadcast_to(part_sum, (1, 128))
+    lane = lax.broadcasted_iota(jnp.int32, (1, 128), 1)
+    srb[r] = jnp.where(lane == 0, part_sum, col_sum[:, Fb:Fb + 1])
     across_rows(srb, sr_ss, sr_rs)
-    total = sum(srb[k] for k in range(R))[:, 0:1]
-    rms = jnp.sqrt(total / (C * Db * R * Fb))
-    end_ref[0] = jnp.max(jnp.maximum(1.0, rms / CLIP_LEVEL))
-    sent(stb.at[pl.ds(0, devices - 1)], st_ss)
-    arrived(stb.at[pl.ds(0, devices - 1)], st_rs)
-    lane = lax.broadcasted_iota(jnp.int32, (1, 128), 1)
-    totals = jnp.sum(stb[...], axis=0)
-    end_ref[1] = jnp.sum(jnp.where(lane == 1, totals, 0.0)) / batch
+    totals = sum(srb[k] for k in range(R))
+    rms = jnp.sqrt(totals / (C * Db * R * Fb))
+    end_v[...] = jnp.where(lane == 0, jnp.maximum(1.0, rms / CLIP_LEVEL), totals / batch)
+    store = pltpu.make_async_copy(end_v, end_ref, ld.at[9])
+    store.start()
+    finish.append(store.wait)
     for wait in finish:
         wait()
 
 
 def divide(raw_ref, row_ref, col_ref, end_ref, upd_ref, nr_ref, nc_ref, loss_ref):
-    upd_ref[...] = raw_ref[...] / end_ref[0]
+    upd_ref[...] = raw_ref[...] / end_ref[:, 0:1]
     nr_ref[...] = row_ref[...]
     nc_ref[...] = col_ref[...]
-    loss_ref[0] = end_ref[1]
+    lane = lax.broadcasted_iota(jnp.int32, (1, 128), 1)
+    loss_ref[0] = jnp.sum(jnp.where(lane == 1, end_ref[...], 0.0))
 
 
 def per_device(pooled, hidden, text, weight, row_moment, col_moment, log_scale, bias):
@@ -559,10 +546,10 @@
             jax.ShapeDtypeStruct((Db, Fb), F32),
             jax.ShapeDtypeStruct((Db,), F32),
             jax.ShapeDtypeStruct((Fb,), F32),
-            jax.ShapeDtypeStruct((2,), F32),
+            jax.ShapeDtypeStruct((1, 128), F32),
         ),
         in_specs=[pl.BlockSpec(memory_space=pl.ANY)] * 6 + [smem] * 2,
-        out_specs=(pl.BlockSpec(memory_space=pl.ANY),) * 3 + (smem,),
+        out_specs=(pl.BlockSpec(memory_space=pl.ANY),) * 4,
         scratch_shapes=[
             pltpu.VMEM((T, R * Fb), BF16),
             pltpu.VMEM((Db, Fb), F32),
@@ -593,18 +580,18 @@
             pltpu.VMEM((Db, Fb), F32),
             pltpu.VMEM((Db,), F32),
             pltpu.VMEM((Fb,), F32),
+            pltpu.VMEM((1, 128), F32),
             pltpu.VMEM((R, 1, Db), F32),
-            pltpu.VMEM((C, 1, Fb), F32),
-            pltpu.VMEM((R * C, 1, 128), F32),
+            pltpu.VMEM((C, 1, Fb + 1), F32),
             pltpu.VMEM((C, 1, Fb), F32),
             pltpu.VMEM((R, 1, 128), F32),
             pltpu.VMEM((plane * T, Fb), BF16),
             pltpu.VMEM((L, T, Dp), BF16),
             pltpu.VMEM((plane * T, Dp), BF16),
-            dma(9),
+            dma(10),
             one, one, one, dma(2, Z), dma(Z), dma(2, Z), one, dma(X * C), one, one,
             one, dma(X, 2), one, dma(2), dma(2), dma(2),
-            one, dma(plane), one, dma(2, Z, K), one, one, one, one, one, one,
+            one, dma(plane), one, dma(Z + 1, K), one, one, one, one,
             one, one, one, one, one, one, one, dma(plane),
         ],
         compiler_params=pltpu.CompilerParams(
@@ -621,7 +608,7 @@
             jax.ShapeDtypeStruct((Fb,), F32),
             jax.ShapeDtypeStruct((1,), F32),
         ),
-        in_specs=[vmem] * 3 + [smem],
+        in_specs=[vmem] * 4,
         out_specs=(vmem,) * 3 + (smem,),
     )(*raw)
     return upd, nr, nc, loss[0]

time: 90.2 us -> 89.5 us (level)
  no operation moved by 1% of the time
where the time goes in v6:
time: 89.5 us; the launch traced here: 89.3 us
  Pallas kernels  87.4 us (98%)
  between operations  1.93 us (2%)
    pallas_call x1, Pallas kernels, per_device(): pl.pallas_call(functools.partial(kernel, sizes), out_shape=(jax.ShapeDtyp...  85.3 us
    pallas_call x1, Pallas kernels, per_device(): pl.pallas_call(divide, out_shape=(jax.ShapeDtypeStruct((Db, Fb), F32), ja...  2.1 us

profile of v6, /device:TPU:0, one launch (start us, length us, event | category | flops | bytes accessed | tf_op | source)
XLA Modules:
  0.0 89.3 jit_solution(13324860153158869851)
XLA Ops:
  1.9 85.3 %shard_map.111 = (f32[144,1076]{1,0:T(8,128)}, f32[144]{0:T(256)}, f32[1076]{0:T(1024)}, f32[1,128]{1,0:T(1,128)}) custom-call(bf16[64,4304]{1,0:T(8,128)(2,1)} %hid_in.1, f32[144,1076]{1,0:T(8,128)} %w_in.1, bf16[64,1152]{1,0:T(8,128)(2,1)} %pool_in.1, bf16[64,1152]{1,0:T(8,128)(2,1)} %text_in.1, f32[144]{0:T(256)} %rm_in.1, f32[1076]{0:T(1024)} %cm_in.1, ...), custom_call_target="tpu_custom_call" | custom-call | tf_op jit(solution)/shard_map/pallas_call | solution.py:543
  87.2 2.1 %shard_map.112 = (f32[144,1076]{1,0:T(8,128)}, f32[144]{0:T(256)}, f32[1076]{0:T(1024)}, f32[1]{0:T(128)}) custom-call(f32[144,1076]{1,0:T(8,128)} %get-tuple-element.12.raw_ref, f32[144]{0:T(256)} %get-tuple-element.13.row_ref, f32[1076]{0:T(1024)} %get-tuple-element.14.col_ref, f32[1,128]{1,0:T(1,128)} %get-tuple-element.15.end_ref), custom_call_target="tpu_custom_call" | custom-call | tf_op jit(solution)/shard_map/pallas_call | solution.py:603

commit v7 on v6

--- a/solution.py
+++ b/solution.py
@@ -156,8 +156,9 @@
     low = z < Z // 2
     final = jnp.where(low, Z - 1, 0)
     edge = jnp.logical_and(E > 0, jnp.logical_or(z == 0, z == Z - 1))
-    nearby = jnp.logical_and(E > 0, jnp.logical_or(z == 1, z == Z - 2))
-    nest = jnp.where(low, 1, Z - 2)
+    nearby = jnp.logical_and(E > 0, jnp.logical_or(z == 2, z == Z - 3))
+    nest = jnp.where(low, 2, Z - 3)
+    theirs_far = jnp.where(z == 2, Z - 1, 0)
 
     def relay(s):
         split = T // 4 if s < 2 else T // 2
@@ -264,6 +265,9 @@
         start, width = spans[g]
         arrived(part.at[pl.ds(0, (X * L - 1) * T), pl.ds(start, width)], p_rs.at[g])
 
+    def hidden_in():
+        arrived(hid.at[pl.ds(0, (plane - 1 - crossing) * T)], hid_rs)
+
     for s in range(1, Z):
         texts_on(s)
         if s == 1:
@@ -274,10 +278,10 @@
             weights_on(s)
         relay(s - 1)
         if s == Z - 2:
-            arrived(hid.at[pl.ds(0, (plane - 1 - crossing) * T)], hid_rs)
+            hidden_in()
+            project(0)
             if E:
                 send(hid, hid2, hf_ss, hf_rs, (r, nest * L + y), edge)
-            project(0)
     weights_on(Z - 1)
     project(1)
     sent(part.at[pl.ds(0, X * L * T)], pp_ss)
@@ -341,7 +345,7 @@
     inner = jnp.sum(unit * ug, axis=1, keepdims=True)
     mg = ((ug - unit * inner) / length).astype(BF16)
     for h in range(L):
-        mg_s[h] = mg[:, h * F2:(h + 1) * F2]
+        mg_s[h, :, :F2] = mg[:, h * F2:(h + 1) * F2]
     others = [
         (lax.rem(x + ox, X), lax.rem(y + oy, L))
         for ox in reversed(range(X)) for oy in reversed(range(L)) if ox or oy
@@ -351,33 +355,52 @@
         for h in range(L):
             top = mg[:, h * F2 + (Z - 1) * Dp:h * F2 + Z * Dp]
             mgx_s[h] = jnp.where(low, top, mg[:, h * F2:h * F2 + Dp])
+    mga[rows(q, T)] = mg_s[y]
+    loss_local = jnp.sum(loss_a + loss_b, axis=0, keepdims=True)
+    csb[c, :, Fb:Fb + 1] = loss_local
+    def far_out():
         for x2, y2 in everyone:
             send(
                 mgx_s.at[y2], mgx.at[rows(q, T)], mgx_ss, mgx_rs.at[q],
-                (x2 * CORES + core, nest * L + y2), edge, True,
+                (x2 * CORES + core, nest * L + y2), bulk=True,
             )
-    for x2, y2 in others:
-        send(
-            mg_s.at[y2], mga.at[rows(q, T)], mg_ss, mg_rs.at[q],
-            (x2 * CORES + core, z * L + y2), bulk=True,
-        )
-    send(mg_s.at[y], mga.at[rows(q, T)], mg_ss, mg_rs.at[q], partner, bulk=True)
-    mga[rows(q, T)] = mg_s[y]
-    loss_local = jnp.sum(loss_a + loss_b, axis=0, keepdims=True)
-    csb[c, :, Fb:Fb + 1] = loss_local
-    for x2, y2 in others:
-        source = (x2 * CORES + core) * L + y2
-        at = mga.at[rows(source, T)]
-        arrived(at, mg_rs.at[source])
-        send(at, at, mg_ss, mg_rs.at[source], partner, bulk=True)
-    sent(mga.at[pl.ds(0, (plane - 1) * T)], mg_ss)
+
+    def exchange(lanes, also=None):
+        for x2, y2 in others:
+            send(
+                mg_s.at[y2, :, lanes], mga.at[rows(q, T), lanes], mg_ss, mg_rs.at[q],
+                (x2 * CORES + core, z * L + y2), bulk=True,
+            )
+        send(mg_s.at[y, :, lanes], mga.at[rows(q, T), lanes], mg_ss, mg_rs.at[q], partner, bulk=True)
+        if also is not None:
+            also()
+        for x2, y2 in others:
+            source = (x2 * CORES + core) * L + y2
+            at = mga.at[rows(source, T), lanes]
+            arrived(at, mg_rs.at[source])
+            send(at, at, mg_ss, mg_rs.at[source], partner, bulk=True)
+        for x2, y2 in [(x, y)] + others:
+            source = (x2 * CORES + 1 - core) * L + y2
+            arrived(mga.at[rows(source, T), lanes], mg_rs.at[source])
+
+    def exchanged(lanes):
+        arrived(mga.at[pl.ds(0, (plane - 1) * T), lanes], mg_ss)
+
+    every = pl.ds(0, F2p)
+    if E:
+        most = max(-(-(F2 - Dp) // 128) * 128, F2p - Dp // 128 * 128)
+        needed = pl.ds(pl.multiple_of(jnp.where(low, 0, F2p - most), 128), most)
+        pl.when(edge)(lambda: exchange(needed, far_out))
+        pl.when(jnp.logical_not(edge))(lambda: exchange(every))
+        finish.append(lambda: pl.when(edge)(lambda: exchanged(needed)))
+        finish.append(lambda: pl.when(jnp.logical_not(edge))(lambda: exchanged(every)))
+    else:
+        exchange(every)
+        finish.append(lambda: exchanged(every))
     if E:
         finish.append(lambda: pl.when(jnp.logical_or(edge, nearby))(
             lambda: arrived(mgx.at[pl.ds(0, X * L * T)], mgx_ss)
         ))
-    for x2, y2 in [(x, y)] + others:
-        source = (x2 * CORES + 1 - core) * L + y2
-        arrived(mga.at[rows(source, T)], mg_rs.at[source])
 
     turned[...] = mga[...].T
 
@@ -393,7 +416,7 @@
         for x2, y2 in everyone:
             source = (x2 * CORES + 1 - core) * L + y2
             arrived(mgx.at[rows(source, T)], mgx_rs.at[source])
-        gp[final] = gp[final] + jnp.dot(mgx[...].T, hid2[...], preferred_element_type=F32)
+        gp[theirs_far] = gp[theirs_far] + jnp.dot(mgx[...].T, hid2[...], preferred_element_type=F32)
 
     def pieces(tau, d):
         place = z if d == 0 else Z - 1 - z
@@ -445,7 +468,7 @@
         return _
 
     steps_g = max((Z - 1) * K + 1 - 2 * E, K - 1 + 2 * (Z - 1 - E)) + 1
-    head = min(K, 2)
+    head = 2
 
     def order(k):
         return jnp.where(low, Z - 1 - k, k)
@@ -456,14 +479,16 @@
         pl.when(jnp.logical_not(edge))(lambda: own_part(order(0)))
         for k in range(2, Z):
             own_part(order(k))
-        pl.when(nearby)(far_part)
         finish.append(lambda: pl.when(edge)(lambda: arrived(gz_s.at[pl.ds(0, Z - 2)], g_ss)))
         finish.append(lambda: pl.when(jnp.logical_not(edge))(lambda: arrived(gz_s.at[pl.ds(0, Z - 1)], g_ss)))
     else:
         for k in range(Z):
             own_part(order(k))
         sent(gz_s.at[pl.ds(0, Z - 1)], g_ss)
-    lax.fori_loop(0, steps_g, later, 0)
+    lax.fori_loop(0, head, later, 0)
+    if E:
+        pl.when(nearby)(far_part)
+    lax.fori_loop(head, steps_g, later, 0)
     g = gp[z][:Db]
 
     def across_cols(box, ss, rs):
@@ -532,7 +557,7 @@
     texts = X * C * T
 
     K = 3 if Dp % 48 == 0 else 1
-    E = 1 if Z >= 4 else 0
+    E = 1 if Z == 4 or Z > 5 else 0
     F2p = -(-F2 // 128) * 128
     Fw = max(-(-Dp // 128) * 128, F2p - (F2 - Dp) // 128 * 128)
     sizes = (R, C, X, Z, T, Db, Dp, Fb, K, E, F2, F2p, Fw)
@@ -571,9 +596,9 @@
             pltpu.VMEM((2 * T, L * F2), BF16),
             pltpu.VMEM((T, L * F2), F32),
             pltpu.VMEM((T, L * F2), F32),
-            pltpu.VMEM((L, T, F2), BF16),
-            pltpu.VMEM((plane * T, F2), BF16),
-            pltpu.VMEM((F2, plane * T), BF16),
+            pltpu.VMEM((L, T, F2p), BF16),
+            pltpu.VMEM((plane * T, F2p), BF16),
+            pltpu.VMEM((F2p, plane * T), BF16),
             pltpu.VMEM((Z, Dp, Fb), F32),
             pltpu.VMEM((Z, Dp, Fb), BF16),
             pltpu.VMEM((2, Z, Dp, Fb), BF16),

time: 89.5 us -> 87.8 us (0.981)
  Pallas kernels: 87.4 us -> 85.7 us
    pallas_call x1, Pallas kernels: 85.3 us -> 83.6 us  [per_device(): pl.pallas_call(functools.partial(kernel, sizes), out_shape=(jax.ShapeDtyp...]
where the time goes in v7:
time: 87.8 us; the launch traced here: 87.6 us
  Pallas kernels  85.7 us (98%)
  between operations  1.93 us (2%)
    pallas_call x1, Pallas kernels, per_device(): pl.pallas_call(functools.partial(kernel, sizes), out_shape=(jax.ShapeDtyp...  83.6 us
    pallas_call x1, Pallas kernels, per_device(): pl.pallas_call(divide, out_shape=(jax.ShapeDtypeStruct((Db, Fb), F32), ja...  2.1 us

profile of v7, /device:TPU:0, one launch (start us, length us, event | category | flops | bytes accessed | tf_op | source)
XLA Modules:
  0.0 87.6 jit_solution(5940727692062204450)
XLA Ops:
  1.9 83.6 %shard_map.111 = (f32[144,1076]{1,0:T(8,128)}, f32[144]{0:T(256)}, f32[1076]{0:T(1024)}, f32[1,128]{1,0:T(1,128)}) custom-call(bf16[64,4304]{1,0:T(8,128)(2,1)} %hid_in.1, f32[144,1076]{1,0:T(8,128)} %w_in.1, bf16[64,1152]{1,0:T(8,128)(2,1)} %pool_in.1, bf16[64,1152]{1,0:T(8,128)(2,1)} %text_in.1, f32[144]{0:T(256)} %rm_in.1, f32[1076]{0:T(1024)} %cm_in.1, ...), custom_call_target="tpu_custom_call" | custom-call | tf_op jit(solution)/shard_map/pallas_call | solution.py:568
  85.5 2.1 %shard_map.112 = (f32[144,1076]{1,0:T(8,128)}, f32[144]{0:T(256)}, f32[1076]{0:T(1024)}, f32[1]{0:T(128)}) custom-call(f32[144,1076]{1,0:T(8,128)} %get-tuple-element.12.raw_ref, f32[144]{0:T(256)} %get-tuple-element.13.row_ref, f32[1076]{0:T(1024)} %get-tuple-element.14.col_ref, f32[1,128]{1,0:T(1,128)} %get-tuple-element.15.end_ref), custom_call_target="tpu_custom_call" | custom-call | tf_op jit(solution)/shard_map/pallas_call | solution.py:628
